TPU v7x, 32 devices: a whole 2x2x4 slice. The times are simulated.
32 devices in a mesh: groups: 2 (over y), space: 4 (over z), rhs: 4 (over x, core).
Axes of the slice: x: 2, y: 2, z: 4, core: 2. Of those that a mesh axis runs over, the one named last changes fastest.
Arguments:
- conductance: float32 [64, 1024], P(('groups', 'space')), parts along dimension 0, may hold values from 0.05 to 2
- nodata: int32 [64, 1024], P(('groups', 'space')), parts along dimension 0, may hold values 0 or 1
- ground_mask: int32 [64, 1024], P(('groups', 'space')), parts along dimension 0, may hold values 0 or 1
- ground_value: float32 [64, 1024], P(('groups', 'space')), parts along dimension 0, may hold values from 0.5 to 4
- source_mask: int32 [64, 1024], P(('groups', 'space')), parts along dimension 0, may hold values 0 or 1
- source_current: float32 [64, 1024], P(('groups', 'space')), parts along dimension 0, may hold values from 0.5 to 4
- tile_inverse: float32 [64, 8, 128, 128], P(('groups', 'space')), parts along dimension 0, may hold values from -0.04 to 8, as said below
- focal_cells: int32 [512, 2], P(('groups', 'rhs')), parts along dimension 0, may hold values from 0 to 32767
Outputs:
- solution: float32 [256, 64, 1024], P('rhs', ('groups', 'space')), parts along dimension 1
- residual: float32 [256, 64, 1024], P('rhs', ('groups', 'space')), parts along dimension 1
There are 2 independent parts, one for each index of `groups`. A program takes and returns all parts, laid end to end along the dimension named above; each array names one. Nothing has to cross between parts.
Inputs may be any that keep to these rules, and one draw needn't show every extreme that they name: `tile_inverse`: each block is symmetric positive definite.
All inputs are finite; a program needn't handle non-finite values. No bound on the sum of `nodata` or of `ground_mask` or of `source_mask` on one device may be relied on, other than what follows from the above.
Results may differ from a plain program's by a relative error of at most 0.00025.
Values sent between devices are 32-bit elements; how exact they have to be, the bound alone decides.
A program may use at most 64 MiB of HBM per device.

v0:
```python
import functools

import jax
import jax.numpy as jnp
from jax import lax
from jax.experimental import pallas as pl
from jax.experimental.pallas import tpu as pltpu
from jax.sharding import PartitionSpec as P

LEAKAGE = 0.05
FOCAL_CURRENT = 16.0
LANES = 128
EXTRA = 8
F32 = jnp.float32
BF16 = jnp.bfloat16


def fold(x):
    out = x[:, :LANES]
    for c in range(1, x.shape[1] // LANES):
        out = out + x[:, c * LANES:(c + 1) * LANES]
    return out


def krylov_kernel(
    count, cond_hbm, nodata_hbm, gmask_hbm, gval_hbm, smask_hbm, scur_hbm, t_hbm, focal_hbm,
    r0_ref, q_ref, w_ref, z_ref, y_ref, coef_ref,
    cond_ref, nodata_ref, gmask_ref, gval_ref, smask_ref, scur_ref, focal_ref, t_ref,
    thl_ref, wts_ref, qhalo_ref, zhalo_ref, msg_ref, got_ref, tmsg_ref, tgot_ref, zmsg_ref, zgot_ref,
    acc_ref, stat_ref, all_ref, late_ref, lates_ref,
    send1, recv1, sendt, recvt, send2, recv2, send3, recv3, send4, recv4, sem_in, sem_t,
):
    rows, cols = cond_ref.shape
    tiles = cols // LANES
    pairs = focal_ref.shape[1]
    ext = pairs + EXTRA
    me = lax.axis_index("space")
    last = count - 1

    barrier = pltpu.get_barrier_semaphore()
    for off in range(1, count):
        pl.semaphore_signal(
            barrier, inc=1, device_id={"space": lax.rem(me + off, count)},
            device_id_type=pl.DeviceIdType.MESH,
        )

    loads = [
        pltpu.make_async_copy(src, dst, sem_in.at[i])
        for i, (src, dst) in enumerate((
            (focal_hbm, focal_ref), (smask_hbm, smask_ref), (scur_hbm, scur_ref),
            (cond_hbm, cond_ref), (nodata_hbm, nodata_ref), (gmask_hbm, gmask_ref),
            (gval_hbm, gval_ref),
        ))
    ]

    def t_load(r):
        return pltpu.make_async_copy(t_hbm.at[r], t_ref.at[r], sem_t.at[r])

    for load in loads:
        load.start()
    for r in (0, rows - 1):
        t_load(r).start()
    for load in loads:
        load.wait()
    for r in range(1, rows - 1):
        t_load(r).start()

    valid = (1 - nodata_ref[...]).astype(F32)
    active = cond_ref[...] * valid
    background = smask_ref[...].astype(F32) * scur_ref[...]

    def edge(a, b, v, u):
        return 0.5 * (a + b) * v * u

    def set_weights():
        grounded = gmask_ref[...].astype(F32) * gval_ref[...]
        lane = lax.broadcasted_iota(jnp.int32, (rows, cols), 1)
        row = lax.broadcasted_iota(jnp.int32, (rows, cols), 0)

        def shifted(x, at, by, axis, edge_at):
            return jnp.where(at == edge_at, 0.0, pltpu.roll(x, by, axis))

        nw, sw, ww, ew = (
            edge(active, shifted(active, *how), valid, shifted(valid, *how))
            for how in ((row, 1, 0, 0), (row, rows - 1, 0, rows - 1),
                        (lane, 1, 1, 0), (lane, cols - 1, 1, cols - 1))
        )
        dg = valid * (LEAKAGE + grounded) + (1.0 - valid) + nw + sw + ww + ew
        for r in range(rows):
            for i, x in enumerate((dg, nw, sw, ww, ew, 0.5 * dg)):
                wts_ref[r, i:i + 1, :] = x[r:r + 1, :]

    acc_ref[...] = jnp.zeros(acc_ref.shape, F32)
    diagonal = lax.broadcasted_iota(jnp.int32, (ext, pairs), 0) == lax.broadcasted_iota(
        jnp.int32, (ext, pairs), 1)
    is_pair = lax.broadcasted_iota(jnp.int32, (ext, 1), 0) < pairs

    def column(i):
        line = jnp.broadcast_to(focal_ref[i:i + 1, :].astype(F32), (ext, pairs))
        at = jnp.sum(jnp.where(diagonal, line, 0.0), 1, keepdims=True).astype(jnp.int32)
        return jnp.where(is_pair, at, -1)

    fa, fb = column(0), column(1)

    def right_side(r):
        ids = (me * rows + r) * cols + lax.broadcasted_iota(jnp.int32, (ext, cols), 1)
        onehot = (ids == fa).astype(F32) - (ids == fb).astype(F32)
        r0_ref[r] = background[r:r + 1, :] + FOCAL_CURRENT * onehot

    right_side(0)
    right_side(rows - 1)

    def precond_row(src, dst, r, split):
        for c in range(tiles):
            cut = slice(c * LANES, (c + 1) * LANES)
            if split:
                t = t_ref[r, c]
                thi = t.astype(BF16)
                thl_ref[r, c, :, :LANES] = thi
                thl_ref[r, c, :, LANES:] = (t - thi.astype(F32)).astype(BF16)
            x = src[r, :, cut]
            hi = x.astype(BF16).astype(F32)
            lhs = jnp.concatenate([hi, x - hi], 0).astype(BF16)
            o = jnp.dot(lhs, thl_ref[r, c], preferred_element_type=F32)
            dst[r, :, cut] = o[:ext, :LANES] + (o[:ext, LANES:] + (o[ext:, :LANES] + o[ext:, LANES:]))

    def precond_inner(src, dst, split):
        def body(r, carry):
            if split:
                t_load(r).wait()
            precond_row(src, dst, r, split)
            return carry
        lax.fori_loop(1, rows - 1, body, 0)

    def over_groups(number, body):
        def step(g, carry):
            body(pl.ds(pl.multiple_of(g * 8, 8), 8))
            return carry
        lax.fori_loop(0, number, step, 0, unroll=next(u for u in (4, 3, 2, 1) if number % u == 0))

    def apply_row(src, dst, r, north, south, number, first=None, second=None):
        def body(s):
            ce = src[r, s, :]
            out = wts_ref[r, 0:1, :] * ce
            if north is not None:
                out = out - wts_ref[r, 1:2, :] * north[0][north[1], s, :]
            if south is not None:
                out = out - wts_ref[r, 2:3, :] * south[0][south[1], s, :]
            out = (
                out
                - wts_ref[r, 3:4, :] * pltpu.roll(ce, 1, 1)
                - wts_ref[r, 4:5, :] * pltpu.roll(ce, cols - 1, 1)
            )
            dst[r, s, :] = out
            if first is not None:
                acc_ref[0, s, :] += fold(first[r, s, :] * ce)
            if second:
                acc_ref[1, s, :] += fold(ce * out)
        over_groups(number, body)

    def apply_inner(src, dst, number, first=None, second=None):
        def body(r, carry):
            apply_row(src, dst, r, (src, r - 1), (src, r + 1), number, first, second)
            return carry
        lax.fori_loop(1, rows - 1, body, 0)

    def moment_row(r, north):
        def body(s):
            z = z_ref[r, s, :]
            t = wts_ref[r, 5:6, :] * z - wts_ref[r, 3:4, :] * pltpu.roll(z, 1, 1)
            if north:
                t = t - wts_ref[r, 1:2, :] * z_ref[r - 1, s, :]
            acc_ref[2, s, :] += fold(w_ref[r, s, :] * z)
            acc_ref[3, s, :] += fold(t * z)
        over_groups(pairs // 8, body)

    def side_copy(src, dst, ssem, rsem, side):
        return pltpu.make_async_remote_copy(
            src_ref=src.at[side], dst_ref=dst.at[1 - side],
            send_sem=ssem.at[side], recv_sem=rsem.at[1 - side],
            device_id={"space": me - 1 if side == 0 else me + 1},
            device_id_type=pl.DeviceIdType.MESH,
        )

    has = (me > 0, me < last)

    def done(src, dst, ssem, rsem):
        for side in range(2):
            @pl.when(has[side])
            def _():
                side_copy(src, dst, ssem, rsem, side).wait_send()
                pltpu.make_async_remote_copy(
                    src_ref=src.at[1 - side], dst_ref=dst.at[side],
                    send_sem=ssem.at[1 - side], recv_sem=rsem.at[side],
                    device_id={"space": me - 1 if side == 0 else me + 1},
                    device_id_type=pl.DeviceIdType.MESH,
                ).wait_recv()

    for r in (0, rows - 1):
        t_load(r).wait()
        precond_row(r0_ref, q_ref, r, True)

    tile_a = lax.shift_right_logical(fa[:pairs] & (cols - 1), 7)
    tile_b = lax.shift_right_logical(fb[:pairs] & (cols - 1), 7)

    def pack(src, r, dst, side):
        va = src[r, :pairs, 0:LANES]
        vb = va
        for c in range(1, tiles):
            x = src[r, :pairs, c * LANES:(c + 1) * LANES]
            va = jnp.where(tile_a == c, x, va)
            vb = jnp.where(tile_b == c, x, vb)
        dst[side, 0:pairs, :] = va
        dst[side, pairs:2 * pairs, :] = vb
        for c in range(tiles):
            at = 2 * pairs + c
            dst[side, at:at + 1, :] = src[r, pairs:pairs + 1, c * LANES:(c + 1) * LANES]

    ends = ((0, 0), (1, rows - 1))
    for side, r in ends:
        pack(q_ref, r, msg_ref, side)
        for c in range(tiles):
            cut = slice(c * LANES, (c + 1) * LANES)
            at = 2 * pairs + c
            msg_ref[side, at + tiles:at + tiles + 1, :] = active[r:r + 1, cut]
            msg_ref[side, at + 2 * tiles:at + 2 * tiles + 1, :] = valid[r:r + 1, cut]
            tmsg_ref[side, c:c + 1, :] = t_ref[r, c, 0:1, :]
            tmsg_ref[side, tiles + c:tiles + c + 1, :] = t_ref[r, c, LANES - 1:LANES, :]

    pl.semaphore_wait(barrier, last)
    for side in range(2):
        @pl.when(has[side])
        def _():
            side_copy(msg_ref, got_ref, send1, recv1, side).start()
            side_copy(tmsg_ref, tgot_ref, sendt, recvt, side).start()

        @pl.when(jnp.logical_not(has[side]))
        def _():
            for ref in (got_ref, tgot_ref, zgot_ref):
                ref[side] = jnp.zeros(ref.shape[1:], F32)

    set_weights()
    for r in range(1, rows - 1):
        right_side(r)
    precond_inner(r0_ref, q_ref, True)
    apply_inner(q_ref, w_ref, ext // 8, r0_ref, True)
    apply_row(q_ref, w_ref, 0, None, (q_ref, 1), ext // 8, r0_ref)
    apply_row(q_ref, w_ref, rows - 1, (q_ref, rows - 2), None, ext // 8, r0_ref)

    done(msg_ref, got_ref, send1, recv1)

    def row_of(side, base):
        return jnp.concatenate([got_ref[side, base + c:base + c + 1, :] for c in range(tiles)], 1)

    halo_a = [row_of(side, 2 * pairs + tiles) for side in range(2)]
    halo_v = [row_of(side, 2 * pairs + 2 * tiles) for side in range(2)]
    for side, r in ends:
        i = 1 + side
        h = edge(active[r:r + 1, :], halo_a[side], valid[r:r + 1, :], halo_v[side])
        wts_ref[r, i:i + 1, :] = h
        wts_ref[r, 0:1, :] += h
        wts_ref[r, 5:6, :] += 0.5 * h
        va = got_ref[side, 0:pairs, :]
        vb = got_ref[side, pairs:2 * pairs, :]
        dots = jnp.zeros((pairs, LANES), F32)
        for c in range(tiles):
            cut = slice(c * LANES, (c + 1) * LANES)
            common = got_ref[side, 2 * pairs + c:2 * pairs + c + 1, :]
            qh = jnp.where(
                tile_a == c, va, jnp.where(tile_b == c, vb, jnp.broadcast_to(common, va.shape))
            )
            qhalo_ref[side, :, cut] = qh - common
            q0 = q_ref[r, :pairs, cut]
            w0 = w_ref[r, :pairs, cut] + h[:, cut] * (q0 - qh)
            w_ref[r, :pairs, cut] = w0
            w_ref[r, pairs:ext, cut] += h[:, cut] * (q_ref[r, pairs:ext, cut] - common)
            dots = dots + q0 * w0
        acc_ref[1, :pairs, :] += dots

    precond_row(w_ref, z_ref, 0, False)
    precond_row(w_ref, z_ref, rows - 1, False)
    for side, r in ends:
        pack(z_ref, r, zmsg_ref, side)
    for side in range(2):
        @pl.when(has[side])
        def _():
            side_copy(zmsg_ref, zgot_ref, send2, recv2, side).start()

    precond_inner(w_ref, z_ref, False)
    moment_row(0, False)

    def moments(r, carry):
        moment_row(r, True)
        return carry

    lax.fori_loop(1, rows, moments, 0)

    lane = lax.broadcasted_iota(jnp.int32, (LANES, LANES), 1)
    pad = jnp.zeros((LANES - pairs, 1), F32)

    def lines(sums):
        table = jnp.zeros((LANES, LANES), F32)
        for i, x in enumerate(sums):
            col = jnp.concatenate([jnp.sum(x, 1, keepdims=True), pad], 0)
            table = jnp.where(lane == i, jnp.broadcast_to(col, table.shape), table)
        return table.T[0:8, :]

    def exchange(src, dst, ssem, rsem):
        return [
            pltpu.make_async_remote_copy(
                src_ref=src, dst_ref=dst.at[k - 1],
                send_sem=ssem.at[k - 1], recv_sem=rsem.at[k - 1],
                device_id={"space": lax.rem(me + k, count)}, device_id_type=pl.DeviceIdType.MESH,
            )
            for k in range(1, count)
        ]

    early = lines([acc_ref[i, :pairs, :] for i in range(4)])
    stat_ref[...] = early
    early_copies = exchange(stat_ref, all_ref, send3, recv3)
    for copy in early_copies:
        copy.start()

    done(tmsg_ref, tgot_ref, sendt, recvt)
    for side in range(2):
        between = edge(halo_a[side][:, :-1], halo_a[side][:, 1:], halo_v[side][:, :-1], halo_v[side][:, 1:])
        for c in range(tiles):
            cut = slice(c * LANES, (c + 1) * LANES)
            near = jnp.zeros((pairs, LANES), F32)
            if c > 0:
                at = c * LANES - 1
                near = near - (between[:, at:at + 1] * qhalo_ref[side, :, at:at + 1]) * tgot_ref[side, c:c + 1, :]
            if c < tiles - 1:
                at = (c + 1) * LANES
                near = near - (between[:, at - 1:at] * qhalo_ref[side, :, at:at + 1]) * tgot_ref[
                    side, tiles + c:tiles + c + 1, :]
            zhalo_ref[side, :, cut] = near

    done(zmsg_ref, zgot_ref, send2, recv2)
    coupling = []
    for side, r in ends:
        va = zgot_ref[side, 0:pairs, :]
        vb = zgot_ref[side, pairs:2 * pairs, :]
        total = jnp.zeros((pairs, LANES), F32)
        for c in range(tiles):
            cut = slice(c * LANES, (c + 1) * LANES)
            other = zgot_ref[side, 2 * pairs + c:2 * pairs + c + 1, :] + zhalo_ref[side, :, cut]
            zh = jnp.where(tile_a == c, va, jnp.where(tile_b == c, vb, other))
            zhalo_ref[side, :, cut] = zh
            total = total + wts_ref[r, 1 + side:2 + side, cut] * z_ref[r, :pairs, cut] * zh
        coupling.append(total)
    late = lines(coupling)
    late_ref[...] = late
    late_copies = exchange(late_ref, lates_ref, send4, recv4)
    for copy in late_copies:
        copy.start()

    apply_inner(z_ref, y_ref, pairs // 8)
    apply_row(z_ref, y_ref, 0, (zhalo_ref, 0), (z_ref, 1), pairs // 8)
    apply_row(z_ref, y_ref, rows - 1, (z_ref, rows - 2), (zhalo_ref, 1), pairs // 8)

    for copy in early_copies:
        copy.wait()
    total = early
    for k in range(1, count):
        total = total + all_ref[k - 1]
    for copy in late_copies:
        copy.wait()
    joint = late[0:1, :] + late[1:2, :]
    for k in range(1, count):
        joint = joint + jnp.where(k <= me, lates_ref[k - 1, 0:1, :], lates_ref[k - 1, 1:2, :])
    gamma0, kappa, mu, half = (total[i:i + 1, :] for i in range(4))
    nu = 2.0 * (half - joint)
    a0 = gamma0 / kappa
    gamma1 = a0 * a0 * mu - gamma0
    beta = gamma1 / gamma0
    a1 = gamma1 / (kappa - 2.0 * a0 * mu + a0 * a0 * nu - beta * gamma1 / a0)
    first = a0 + a1 * (1.0 + beta)
    both = jnp.concatenate([first, a0 * a1, jnp.zeros((LANES - 2, LANES), F32)], 0).T
    lane_p = lax.broadcasted_iota(jnp.int32, (pairs, LANES), 1)
    coef_ref[...] = jnp.where(lane_p < LANES // 2, both[:pairs, 0:1], both[:pairs, 1:2])


def combine_kernel(coef_ref, r0_ref, q_ref, w_ref, z_ref, y_ref, sol_hbm, res_hbm, sol_ref, res_ref, sem):
    pairs, rows, cols = sol_ref.shape
    block = 8

    def out(i, src, dst, k):
        cut = pl.ds(pl.multiple_of(i * block, block), block)
        return pltpu.make_async_copy(src.at[cut], dst.at[cut], sem.at[k, i])

    def body(i, carry):
        cut = pl.ds(pl.multiple_of(i * block, block), block)
        one = coef_ref[cut, 0:1]
        two = coef_ref[cut, LANES - 1:LANES]
        for r in range(rows):
            sol_ref[cut, r, :] = one * q_ref[r, cut, :] - two * z_ref[r, cut, :]
            res_ref[cut, r, :] = r0_ref[r, cut, :] - one * w_ref[r, cut, :] + two * y_ref[r, cut, :]
        out(i, sol_ref, sol_hbm, 0).start()
        out(i, res_ref, res_hbm, 1).start()
        return carry

    lax.fori_loop(0, pairs // block, body, 0)

    def finish(i, carry):
        out(i, sol_ref, sol_hbm, 0).wait()
        out(i, res_ref, res_hbm, 1).wait()
        return carry

    lax.fori_loop(0, pairs // block, finish, 0)


def on_device(count, cond, nodata, gmask, gval, smask, scur, tinv, focal):
    rows, cols = cond.shape
    pairs = focal.shape[0]
    tiles = cols // LANES
    ext = pairs + EXTRA
    field = jax.ShapeDtypeStruct((rows, ext, cols), F32)
    vm = pl.BlockSpec(memory_space=pltpu.VMEM)
    hbm = pl.BlockSpec(memory_space=pltpu.HBM)
    msg = (2, 2 * pairs + 3 * tiles, LANES)
    tmsg = (2, 2 * tiles, LANES)
    zmsg = (2, 2 * pairs + tiles, LANES)
    others = count - 1
    small = (rows, cols)
    r0, q, w, z, y, coef = pl.pallas_call(
        functools.partial(krylov_kernel, count),
        out_shape=[field] * 5 + [jax.ShapeDtypeStruct((pairs, LANES), F32)],
        in_specs=[hbm] * 8,
        out_specs=[vm] * 6,
        scratch_shapes=[
            pltpu.VMEM(small, F32),
            pltpu.VMEM(small, jnp.int32),
            pltpu.VMEM(small, jnp.int32),
            pltpu.VMEM(small, F32),
            pltpu.VMEM(small, jnp.int32),
            pltpu.VMEM(small, F32),
            pltpu.VMEM((2, pairs), jnp.int32),
            pltpu.VMEM(tinv.shape, F32),
            pltpu.VMEM((rows, tiles, LANES, 2 * LANES), BF16),
            pltpu.VMEM((rows, 8, cols), F32),
            pltpu.VMEM((2, pairs, cols), F32),
            pltpu.VMEM((2, pairs, cols), F32),
            pltpu.VMEM(msg, F32),
            pltpu.VMEM(msg, F32),
            pltpu.VMEM(tmsg, F32),
            pltpu.VMEM(tmsg, F32),
            pltpu.VMEM(zmsg, F32),
            pltpu.VMEM(zmsg, F32),
            pltpu.VMEM((4, ext, LANES), F32),
            pltpu.VMEM((8, LANES), F32),
            pltpu.VMEM((others, 8, LANES), F32),
            pltpu.VMEM((8, LANES), F32),
            pltpu.VMEM((others, 8, LANES), F32),
            *[pltpu.SemaphoreType.DMA((2,))] * 6,
            *[pltpu.SemaphoreType.DMA((others,))] * 4,
            pltpu.SemaphoreType.DMA((7,)),
            pltpu.SemaphoreType.DMA((rows,)),
        ],
        compiler_params=pltpu.CompilerParams(
            collective_id=0, has_side_effects=True, vmem_limit_bytes=36 * 1024 * 1024
        ),
        name="krylov",
    )(*(
        pltpu.with_memory_space_constraint(x, pltpu.HBM)
        for x in (cond, nodata, gmask, gval, smask, scur, tinv, focal.T)
    ))

    out = jax.ShapeDtypeStruct((pairs, rows, cols), F32)
    return tuple(pl.pallas_call(
        combine_kernel,
        out_shape=[out, out],
        in_specs=[vm] * 6,
        out_specs=[hbm, hbm],
        scratch_shapes=[
            pltpu.VMEM(out.shape, F32),
            pltpu.VMEM(out.shape, F32),
            pltpu.SemaphoreType.DMA((2, pairs // 8)),
        ],
        compiler_params=pltpu.CompilerParams(vmem_limit_bytes=20 * 1024 * 1024),
        name="combine",
    )(coef, r0, q, w, z, y))


def solution(mesh):
    return jax.shard_map(
        functools.partial(on_device, mesh.shape["space"]),
        mesh=mesh,
        in_specs=(
            P(("groups", "space"), None),
            P(("groups", "space"), None),
            P(("groups", "space"), None),
            P(("groups", "space"), None),
            P(("groups", "space"), None),
            P(("groups", "space"), None),
            P(("groups", "space"), None, None, None),
            P(("groups", "rhs"), None),
        ),
        out_specs=(P("rhs", ("groups", "space"), None), P("rhs", ("groups", "space"), None)),
        check_vma=False,
    )
```

profile of v0, /device:TPU:0, one launch (start us, length us, event | category | flops | bytes accessed | tf_op | source)
XLA Modules:
  0.0 24.7 jit_solution(16733712038934119068)
XLA Ops:
  0.6 21.0 %krylov.1 = (f32[8,72,1024]{2,1,0:T(8,128)S(1)}, f32[8,72,1024]{2,1,0:T(8,128)S(1)}, f32[8,72,1024]{2,1,0:T(8,128)S(1)}, f32[8,72,1024]{2,1,0:T(8,128)S(1)}, f32...) custom-call(f32[8,1024]{1,0:T(8,128)} %cond_hbm.1, s32[8,1024]{1,0:T(8,128)} %nodata_hbm.1, s32[8,1024]{1,0:T(8,128)} %gmask_hbm.1, ...), custom_call_target="tpu_custom_call" | custom-call | tf_op jit(solution)/shard_map/krylov/pallas_call | solution.py:426
  21.6 3.1 %combine.1 = (f32[64,8,1024]{2,1,0:T(8,128)}, f32[64,8,1024]{2,1,0:T(8,128)}) custom-call(f32[64,128]{1,0:T(8,128)S(1)} %get-tuple-element.8.coef_ref, f32[8,72,1024]{2,1,0:T(8,128)S(1)} %get-tuple-element.9.r0_ref, f32[8,72,1024]{2,1,0:T(8,128)S(1)} %get-tuple-element.10.q_ref, f32[8,72,1024]{2,1,0:T(8,128)S(1)} %get-tuple-element.11.w_ref, ...), custom_call_target="tpu_custom_call" | custom-call | tf_op jit(solution)/shard_map/combine/pallas_call | solution.py:470
where the time goes:
time: 24.9 us; the launch traced here: 24.7 us
  Pallas kernels  24.1 us (97%)
  between operations  0.64 us (3%)
    pallas_call x1, Pallas kernels, on_device(): pl.pallas_call(functools.partial(krylov_kernel, count), out_shape=[field]...  21 us
    pallas_call x1, Pallas kernels, on_device(): pl.pallas_call(combine_kernel, out_shape=[out, out], in_specs=[vm] * 6, o...  3.06 us

commit v1 on v0

v1 whole, which is shorter than its diff:
```python
import functools

import jax
import jax.numpy as jnp
from jax import lax
from jax.experimental import pallas as pl
from jax.experimental.pallas import tpu as pltpu
from jax.sharding import PartitionSpec as P

LEAKAGE = 0.05
FOCAL_CURRENT = 16.0
LANES = 128
EXTRA = 8
F32 = jnp.float32
BF16 = jnp.bfloat16


def krylov_kernel(
    count, cond_hbm, nodata_hbm, gmask_hbm, gval_hbm, smask_hbm, scur_hbm, t_hbm, focal_hbm,
    r0_ref, q_ref, w_ref, z_ref, y_ref, coef_ref,
    cond_ref, nodata_ref, gmask_ref, gval_ref, smask_ref, scur_ref, focal_ref, ids_ref, te_ref, ti_ref,
    thl_ref, wts_ref, spot_ref, qhalo_ref, zhalo_ref, msg_ref, got_ref, bmsg_ref, bgot_ref, tmsg_ref, tgot_ref,
    zmsg_ref, zgot_ref, acc_ref, stat_ref, all_ref, late_ref, lates_ref,
    send1, recv1, sendb, recvb, sendt, recvt, send2, recv2, send3, recv3, send4, recv4, sem_in, sem_t,
):
    rows, cols = cond_ref.shape
    tiles = cols // LANES
    pairs = focal_ref.shape[1]
    ext = pairs + EXTRA
    me = lax.axis_index("space")
    last = count - 1
    ends = ((0, 0), (1, rows - 1))
    inner = range(1, rows - 1)
    cuts = [slice(c * LANES, (c + 1) * LANES) for c in range(tiles)]

    barrier = pltpu.get_barrier_semaphore()
    for off in range(1, count):
        pl.semaphore_signal(
            barrier, inc=1, device_id={"space": lax.rem(me + off, count)},
            device_id_type=pl.DeviceIdType.MESH,
        )

    loads = [
        pltpu.make_async_copy(src, dst, sem_in.at[i])
        for i, (src, dst) in enumerate((
            (focal_hbm, ids_ref), (focal_hbm, focal_ref), (t_hbm.at[0], te_ref.at[pl.ds(0, cols)]),
            (t_hbm.at[rows - 1], te_ref.at[pl.ds(cols, cols)]), (smask_hbm, smask_ref), (scur_hbm, scur_ref),
            (cond_hbm, cond_ref), (nodata_hbm, nodata_ref), (gmask_hbm, gmask_ref), (gval_hbm, gval_ref),
        ))
    ]
    t_loads = [
        pltpu.make_async_copy(t_hbm.at[r], ti_ref.at[pl.ds((r - 1) * cols, cols)], sem_t.at[r]) for r in inner
    ]
    for load in loads:
        load.start()
    for load in loads:
        load.wait()
    for load in t_loads:
        load.start()

    def gather(src, at):
        for p in range(pairs):
            for i in range(2):
                spot_ref[i, p:p + 1, :] = src[pl.ds(at(ids_ref[i, p]), 1), :]
        return FOCAL_CURRENT * spot_ref[0], -FOCAL_CURRENT * spot_ref[1]

    half = (rows * cols // 2).bit_length() - 1
    near_a, near_b = gather(
        te_ref, lambda i: (i & (cols - 1)) + (lax.shift_right_logical(i, half) & 1) * cols)

    diagonal = lax.broadcasted_iota(jnp.int32, (pairs, pairs), 0) == lax.broadcasted_iota(
        jnp.int32, (pairs, pairs), 1)
    lane = lax.broadcasted_iota(jnp.int32, (pairs, LANES), 1)

    def column(i):
        line = jnp.broadcast_to(focal_ref[i:i + 1, :].astype(F32), (pairs, pairs))
        return jnp.broadcast_to(
            jnp.sum(jnp.where(diagonal, line, 0.0), 1, keepdims=True).astype(jnp.int32), (pairs, LANES))

    at_a, at_b = (column(i) - me * (rows * cols) for i in range(2))
    spot_a, spot_b = (lax.shift_right_arithmetic(x, 7) for x in (at_a, at_b))
    tile_a, tile_b = spot_a & (tiles - 1), spot_b & (tiles - 1)

    def within(spot, low, high):
        return jnp.logical_and(spot >= low * tiles, spot < high * tiles)

    for side, r in ends:
        msg_ref[side, 0:pairs, :] = jnp.where(within(spot_a, r, r + 1), near_a, 0.0)
        msg_ref[side, pairs:2 * pairs, :] = jnp.where(within(spot_b, r, r + 1), near_b, 0.0)

    def side_copy(src, dst, ssem, rsem, side):
        return pltpu.make_async_remote_copy(
            src_ref=src.at[side], dst_ref=dst.at[1 - side],
            send_sem=ssem.at[side], recv_sem=rsem.at[1 - side],
            device_id={"space": me - 1 if side == 0 else me + 1},
            device_id_type=pl.DeviceIdType.MESH,
        )

    has = (me > 0, me < last)

    def send(src, dst, ssem, rsem):
        for side in range(2):
            @pl.when(has[side])
            def _():
                side_copy(src, dst, ssem, rsem, side).start()

            @pl.when(jnp.logical_not(has[side]))
            def _():
                dst[side] = jnp.zeros(dst.shape[1:], F32)

    def done(src, dst, ssem, rsem):
        for side in range(2):
            @pl.when(has[side])
            def _():
                side_copy(src, dst, ssem, rsem, side).wait_send()
                pltpu.make_async_remote_copy(
                    src_ref=src.at[1 - side], dst_ref=dst.at[side],
                    send_sem=ssem.at[1 - side], recv_sem=rsem.at[side],
                    device_id={"space": me - 1 if side == 0 else me + 1},
                    device_id_type=pl.DeviceIdType.MESH,
                ).wait_recv()

    pl.semaphore_wait(barrier, last)
    send(msg_ref, got_ref, send1, recv1)

    valid = (1 - nodata_ref[...]).astype(F32)
    active = cond_ref[...] * valid
    background = smask_ref[...].astype(F32) * scur_ref[...]

    def tile_of(r, c):
        if r == 0 or r == rows - 1:
            return te_ref[pl.ds((cols if r else 0) + c * LANES, LANES), :]
        return ti_ref[pl.ds((r - 1) * cols + c * LANES, LANES), :]

    def product(x, r, c):
        number = x.shape[0]
        hi = x.astype(BF16).astype(F32)
        lhs = jnp.concatenate([hi, x - hi], 0).astype(BF16)
        o = jnp.dot(lhs, thl_ref[r, c], preferred_element_type=F32)
        return o[:number, :LANES] + (o[:number, LANES:] + (o[number:, :LANES] + o[number:, LANES:]))

    def shared_row(r):
        dot = jnp.zeros((EXTRA, LANES), F32)
        for c, cut in enumerate(cuts):
            t = tile_of(r, c)
            thi = t.astype(BF16)
            thl_ref[r, c, :, :LANES] = thi
            thl_ref[r, c, :, LANES:] = (t - thi.astype(F32)).astype(BF16)
            x = jnp.broadcast_to(background[r:r + 1, cut], (EXTRA, LANES))
            q = product(x, r, c)
            q_ref[r, pairs:ext, cut] = q
            dot = dot + x * q
        return dot

    shared = shared_row(0) + shared_row(rows - 1)
    for side, r in ends:
        for c, cut in enumerate(cuts):
            bmsg_ref[side, c:c + 1, :] = q_ref[r, pairs:pairs + 1, cut]
            bmsg_ref[side, tiles + c:tiles + c + 1, :] = active[r:r + 1, cut]
            bmsg_ref[side, 2 * tiles + c:2 * tiles + c + 1, :] = valid[r:r + 1, cut]
            first = r and cols
            tmsg_ref[side, c:c + 1, :] = te_ref[first + c * LANES:first + c * LANES + 1, :]
            tmsg_ref[side, tiles + c:tiles + c + 1, :] = te_ref[
                first + c * LANES + LANES - 1:first + (c + 1) * LANES, :]
    send(bmsg_ref, bgot_ref, sendb, recvb)
    send(tmsg_ref, tgot_ref, sendt, recvt)

    def edge(a, b, v, u):
        return 0.5 * (a + b) * v * u

    row_at = lax.broadcasted_iota(jnp.int32, (rows, cols), 0)
    col_at = lax.broadcasted_iota(jnp.int32, (rows, cols), 1)

    def shifted(x, by, axis):
        length = x.shape[axis]
        at = (row_at, col_at)[axis][:x.shape[0], :]
        return jnp.where(at == (0 if by == 1 else length - 1), 0.0, pltpu.roll(x, by % length, axis))

    nw, sw, ww, ew = (
        edge(active, shifted(active, *how), valid, shifted(valid, *how))
        for how in ((1, 0), (-1, 0), (1, 1), (-1, 1))
    )
    dg = valid * (LEAKAGE + gmask_ref[...].astype(F32) * gval_ref[...]) + (1.0 - valid) + nw + sw + ww + ew
    for r in range(rows):
        for i, x in enumerate((dg, nw, sw, ww, ew, 0.5 * dg, background)):
            wts_ref[r, i:i + 1, :] = x[r:r + 1, :]

    for load in t_loads:
        load.wait()
    far_a, far_b = gather(
        ti_ref, lambda i: jnp.clip((i & (rows * cols - 1)) - cols, 0, (rows - 2) * cols - 1))
    for r in inner:
        shared = shared + shared_row(r)

    def dense_row(r, a, b, dot):
        for c, cut in enumerate(cuts):
            k = r * tiles + c
            x = jnp.where(spot_a == k, a, 0.0) + jnp.where(spot_b == k, b, 0.0)
            q_ref[r, 0:pairs, cut] = q_ref[r, pairs:pairs + 1, cut] + x
            dot = dot + background[r:r + 1, cut] * x
        return dot

    dot = jnp.zeros((pairs, LANES), F32)
    for r in range(rows):
        a, b = (far_a, far_b) if r in inner else (near_a, near_b)
        dot = dense_row(r, a, b, dot)
    in_a, in_b = (
        jnp.where(within(spot, 1, rows - 1), far, jnp.where(within(spot, 0, rows), near, 0.0))
        for spot, far, near in ((spot_a, far_a, near_a), (spot_b, far_b, near_b))
    )
    same = spot_a == spot_b
    own = jnp.where(lane == (at_a & (LANES - 1)), in_a + jnp.where(same, in_b, 0.0), 0.0) - jnp.where(
        lane == (at_b & (LANES - 1)), in_b + jnp.where(same, in_a, 0.0), 0.0)
    acc_ref[0] = 2.0 * dot + FOCAL_CURRENT * own + jnp.broadcast_to(shared[0:1, :], dot.shape)
    for i in range(1, 4):
        acc_ref[i] = jnp.zeros(acc_ref.shape[1:], F32)

    parts = [slice(p, p + pairs // 2) for p in (0, pairs // 2)]
    extra = slice(pairs, ext)

    def sides(xs):
        at = lane[:xs[0].shape[0]]
        west = [pltpu.roll(x, 1, 1) for x in xs]
        east = [pltpu.roll(x, LANES - 1, 1) for x in xs]
        west = west[:1] + [jnp.where(at == 0, west[c - 1], west[c]) for c in range(1, tiles)]
        east = [jnp.where(at == LANES - 1, east[c + 1], east[c]) for c in range(tiles - 1)] + east[-1:]
        return west, east

    def apply_part(src, dst, r, s, north, south, acc=None):
        xs = [src[r, s, cut] for cut in cuts]
        west, east = sides(xs)
        dots = None
        for c, cut in enumerate(cuts):
            out = (
                wts_ref[r, 0:1, cut] * xs[c] - wts_ref[r, 3:4, cut] * west[c] - wts_ref[r, 4:5, cut] * east[c]
            )
            if north is not None:
                out = out - wts_ref[r, 1:2, cut] * north[0][north[1], s, cut]
            if south is not None:
                out = out - wts_ref[r, 2:3, cut] * south[0][south[1], s, cut]
            dst[r, s, cut] = out
            dots = xs[c] * out if dots is None else dots + xs[c] * out
        if acc is not None:
            acc_ref[acc, s, :] += dots

    def apply_inner(src, dst, both, acc=None):
        def body(r, carry):
            for s in parts:
                apply_part(src, dst, r, s, (src, r - 1), (src, r + 1), acc)
            if both:
                apply_part(src, dst, r, extra, (src, r - 1), (src, r + 1))
            return carry
        lax.fori_loop(1, rows - 1, body, 0)

    apply_inner(q_ref, w_ref, True, 1)
    for s in (*parts, extra):
        apply_part(q_ref, w_ref, 0, s, None, (q_ref, 1))
        apply_part(q_ref, w_ref, rows - 1, s, (q_ref, rows - 2), None)

    done(msg_ref, got_ref, send1, recv1)
    done(bmsg_ref, bgot_ref, sendb, recvb)

    def row_of(side, base):
        return jnp.concatenate([bgot_ref[side, base + c:base + c + 1, :] for c in range(tiles)], 1)

    halo_a = [row_of(side, tiles) for side in range(2)]
    halo_v = [row_of(side, 2 * tiles) for side in range(2)]
    for side, r in ends:
        i = 1 + side
        h = edge(active[r:r + 1, :], halo_a[side], valid[r:r + 1, :], halo_v[side])
        wts_ref[r, i:i + 1, :] = h
        wts_ref[r, 0:1, :] += h
        wts_ref[r, 5:6, :] += 0.5 * h
        va = got_ref[side, 0:pairs, :]
        vb = got_ref[side, pairs:2 * pairs, :]
        dots = jnp.zeros((pairs, LANES), F32)
        for c, cut in enumerate(cuts):
            common = bgot_ref[side, c:c + 1, :]
            qh = jnp.where(tile_a == c, va, 0.0) + jnp.where(tile_b == c, vb, 0.0)
            qhalo_ref[side, :, cut] = qh
            q0 = q_ref[r, :pairs, cut]
            w0 = w_ref[r, :pairs, cut] + h[:, cut] * (q0 - (qh + common))
            w_ref[r, :pairs, cut] = w0
            w_ref[r, extra, cut] += h[:, cut] * (q_ref[r, extra, cut] - common)
            dots = dots + q0 * w0
        acc_ref[1] += dots

    def precond_row(r):
        for c, cut in enumerate(cuts):
            z_ref[r, :, cut] = product(w_ref[r, :, cut], r, c)

    def pack(src, r, dst, side):
        va = src[r, :pairs, 0:LANES]
        vb = va
        for c in range(1, tiles):
            x = src[r, :pairs, cuts[c]]
            va = jnp.where(tile_a == c, x, va)
            vb = jnp.where(tile_b == c, x, vb)
        dst[side, 0:pairs, :] = va
        dst[side, pairs:2 * pairs, :] = vb
        for c, cut in enumerate(cuts):
            dst[side, 2 * pairs + c:2 * pairs + c + 1, :] = src[r, pairs:pairs + 1, cut]

    precond_row(0)
    precond_row(rows - 1)
    for side, r in ends:
        pack(z_ref, r, zmsg_ref, side)
    send(zmsg_ref, zgot_ref, send2, recv2)

    for r in inner:
        precond_row(r)

    def moment_part(r, s, north):
        zs = [z_ref[r, s, cut] for cut in cuts]
        west, _ = sides(zs)
        mu = nu = None
        for c, cut in enumerate(cuts):
            t = wts_ref[r, 5:6, cut] * zs[c] - wts_ref[r, 3:4, cut] * west[c]
            if north:
                t = t - wts_ref[r, 1:2, cut] * z_ref[r - 1, s, cut]
            one, two = w_ref[r, s, cut] * zs[c], t * zs[c]
            mu, nu = (one, two) if mu is None else (mu + one, nu + two)
        acc_ref[2, s, :] += mu
        acc_ref[3, s, :] += nu

    def moments(r, carry):
        for s in parts:
            moment_part(r, s, True)
        return carry

    for s in parts:
        moment_part(0, s, False)
    lax.fori_loop(1, rows, moments, 0)

    square = lax.broadcasted_iota(jnp.int32, (LANES, LANES), 1)
    pad = jnp.zeros((LANES - pairs, 1), F32)

    def lines(sums):
        table = jnp.zeros((LANES, LANES), F32)
        for i, x in enumerate(sums):
            col = jnp.concatenate([jnp.sum(x, 1, keepdims=True), pad], 0)
            table = jnp.where(square == i, jnp.broadcast_to(col, table.shape), table)
        return table.T[0:8, :]

    def exchange(src, dst, ssem, rsem):
        return [
            pltpu.make_async_remote_copy(
                src_ref=src, dst_ref=dst.at[k - 1],
                send_sem=ssem.at[k - 1], recv_sem=rsem.at[k - 1],
                device_id={"space": lax.rem(me + k, count)}, device_id_type=pl.DeviceIdType.MESH,
            )
            for k in range(1, count)
        ]

    early = lines([acc_ref[i] for i in range(4)])
    stat_ref[...] = early
    early_copies = exchange(stat_ref, all_ref, send3, recv3)
    for copy in early_copies:
        copy.start()

    done(tmsg_ref, tgot_ref, sendt, recvt)
    for side in range(2):
        halo_w, halo_e = (
            edge(halo_a[side], shifted(halo_a[side], by, 1), halo_v[side], shifted(halo_v[side], by, 1))
            for by in (1, -1)
        )
        near = [jnp.zeros((pairs, LANES), F32)] * tiles
        for c, cut in enumerate(cuts):
            qh = qhalo_ref[side, :, cut]
            if c > 0:
                gone = (halo_w[:, cut] * qh)[:, 0:1]
                near[c - 1] = near[c - 1] - gone * tgot_ref[side, tiles + c - 1:tiles + c, :]
            if c < tiles - 1:
                gone = (halo_e[:, cut] * qh)[:, LANES - 1:LANES]
                near[c + 1] = near[c + 1] - gone * tgot_ref[side, c + 1:c + 2, :]
        for c, cut in enumerate(cuts):
            zhalo_ref[side, :, cut] = near[c]

    done(zmsg_ref, zgot_ref, send2, recv2)
    coupling = []
    for side, r in ends:
        va = zgot_ref[side, 0:pairs, :]
        vb = zgot_ref[side, pairs:2 * pairs, :]
        total = jnp.zeros((pairs, LANES), F32)
        for c, cut in enumerate(cuts):
            other = zgot_ref[side, 2 * pairs + c:2 * pairs + c + 1, :] + zhalo_ref[side, :, cut]
            zh = jnp.where(tile_a == c, va, jnp.where(tile_b == c, vb, other))
            zhalo_ref[side, :, cut] = zh
            total = total + wts_ref[r, 1 + side:2 + side, cut] * z_ref[r, :pairs, cut] * zh
        coupling.append(total)
    late = lines(coupling)
    late_ref[...] = late
    late_copies = exchange(late_ref, lates_ref, send4, recv4)
    for copy in late_copies:
        copy.start()

    apply_inner(z_ref, y_ref, False)
    for s in parts:
        apply_part(z_ref, y_ref, 0, s, (zhalo_ref, 0), (z_ref, 1))
        apply_part(z_ref, y_ref, rows - 1, s, (z_ref, rows - 2), (zhalo_ref, 1))

    def right_side(r, carry):
        for c, cut in enumerate(cuts):
            local = r * cols + c * LANES + lane
            x = jnp.where(local == at_a, FOCAL_CURRENT, 0.0) - jnp.where(local == at_b, FOCAL_CURRENT, 0.0)
            r0_ref[r, 0:pairs, cut] = wts_ref[r, 6:7, cut] + x
        return carry

    lax.fori_loop(0, rows, right_side, 0)

    for copy in early_copies:
        copy.wait()
    total = early
    for k in range(1, count):
        total = total + all_ref[k - 1]
    for copy in late_copies:
        copy.wait()
    joint = late[0:1, :] + late[1:2, :]
    for k in range(1, count):
        joint = joint + jnp.where(k <= me, lates_ref[k - 1, 0:1, :], lates_ref[k - 1, 1:2, :])
    gamma0, kappa, mu, part = (total[i:i + 1, :] for i in range(4))
    nu = 2.0 * (part - joint)
    a0 = gamma0 / kappa
    gamma1 = a0 * a0 * mu - gamma0
    beta = gamma1 / gamma0
    a1 = gamma1 / (kappa - 2.0 * a0 * mu + a0 * a0 * nu - beta * gamma1 / a0)
    first = a0 + a1 * (1.0 + beta)
    both = jnp.concatenate([first, a0 * a1, jnp.zeros((LANES - 2, LANES), F32)], 0).T
    coef_ref[...] = jnp.where(lane < LANES // 2, both[:pairs, 0:1], both[:pairs, 1:2])


def combine_kernel(coef_ref, r0_ref, q_ref, w_ref, z_ref, y_ref, sol_hbm, res_hbm, sol_ref, res_ref, sem):
    pairs, rows, cols = sol_ref.shape
    block = 8

    def out(i, src, dst, k):
        cut = pl.ds(pl.multiple_of(i * block, block), block)
        return pltpu.make_async_copy(src.at[cut], dst.at[cut], sem.at[k, i])

    def body(i, carry):
        cut = pl.ds(pl.multiple_of(i * block, block), block)
        one = coef_ref[cut, 0:1]
        two = coef_ref[cut, LANES - 1:LANES]
        for r in range(rows):
            sol_ref[cut, r, :] = one * q_ref[r, cut, :] - two * z_ref[r, cut, :]
            res_ref[cut, r, :] = r0_ref[r, cut, :] - one * w_ref[r, cut, :] + two * y_ref[r, cut, :]
        out(i, sol_ref, sol_hbm, 0).start()
        out(i, res_ref, res_hbm, 1).start()
        return carry

    lax.fori_loop(0, pairs // block, body, 0)

    def finish(i, carry):
        out(i, sol_ref, sol_hbm, 0).wait()
        out(i, res_ref, res_hbm, 1).wait()
        return carry

    lax.fori_loop(0, pairs // block, finish, 0)


def on_device(count, cond, nodata, gmask, gval, smask, scur, tinv, focal):
    rows, cols = cond.shape
    pairs = focal.shape[0]
    tiles = cols // LANES
    ext = pairs + EXTRA
    field = jax.ShapeDtypeStruct((rows, ext, cols), F32)
    vm = pl.BlockSpec(memory_space=pltpu.VMEM)
    hbm = pl.BlockSpec(memory_space=pltpu.HBM)
    msg = (2, 2 * pairs, LANES)
    bmsg = (2, 3 * tiles, LANES)
    tmsg = (2, 2 * tiles, LANES)
    zmsg = (2, 2 * pairs + tiles, LANES)
    others = count - 1
    small = (rows, cols)
    r0, q, w, z, y, coef = pl.pallas_call(
        functools.partial(krylov_kernel, count),
        out_shape=[field] * 5 + [jax.ShapeDtypeStruct((pairs, LANES), F32)],
        in_specs=[hbm] * 8,
        out_specs=[vm] * 6,
        scratch_shapes=[
            pltpu.VMEM(small, F32),
            pltpu.VMEM(small, jnp.int32),
            pltpu.VMEM(small, jnp.int32),
            pltpu.VMEM(small, F32),
            pltpu.VMEM(small, jnp.int32),
            pltpu.VMEM(small, F32),
            pltpu.VMEM((2, pairs), jnp.int32),
            pltpu.SMEM((2, pairs), jnp.int32),
            pltpu.VMEM((2 * cols, LANES), F32),
            pltpu.VMEM(((rows - 2) * cols, LANES), F32),
            pltpu.VMEM((rows, tiles, LANES, 2 * LANES), BF16),
            pltpu.VMEM((rows, 8, cols), F32),
            pltpu.VMEM((2, pairs, LANES), F32),
            pltpu.VMEM((2, pairs, cols), F32),
            pltpu.VMEM((2, pairs, cols), F32),
            *[pltpu.VMEM(shape, F32) for shape in (msg, bmsg, tmsg, zmsg) for _ in range(2)],
            pltpu.VMEM((4, pairs, LANES), F32),
            *[pltpu.VMEM(shape, F32) for _ in range(2) for shape in ((8, LANES), (others, 8, LANES))],
            *[pltpu.SemaphoreType.DMA((2,))] * 8,
            *[pltpu.SemaphoreType.DMA((others,))] * 4,
            pltpu.SemaphoreType.DMA((10,)),
            pltpu.SemaphoreType.DMA((rows,)),
        ],
        compiler_params=pltpu.CompilerParams(
            collective_id=0, has_side_effects=True, vmem_limit_bytes=36 * 1024 * 1024
        ),
        name="krylov",
    )(*(
        pltpu.with_memory_space_constraint(x, pltpu.HBM)
        for x in (cond, nodata, gmask, gval, smask, scur, tinv.reshape(rows, cols, LANES), focal.T)
    ))

    out = jax.ShapeDtypeStruct((pairs, rows, cols), F32)
    return tuple(pl.pallas_call(
        combine_kernel,
        out_shape=[out, out],
        in_specs=[vm] * 6,
        out_specs=[hbm, hbm],
        scratch_shapes=[
            pltpu.VMEM(out.shape, F32),
            pltpu.VMEM(out.shape, F32),
            pltpu.SemaphoreType.DMA((2, pairs // 8)),
        ],
        compiler_params=pltpu.CompilerParams(vmem_limit_bytes=20 * 1024 * 1024),
        name="combine",
    )(coef, r0, q, w, z, y))


def solution(mesh):
    return jax.shard_map(
        functools.partial(on_device, mesh.shape["space"]),
        mesh=mesh,
        in_specs=(
            P(("groups", "space"), None),
            P(("groups", "space"), None),
            P(("groups", "space"), None),
            P(("groups", "space"), None),
            P(("groups", "space"), None),
            P(("groups", "space"), None),
            P(("groups", "space"), None, None, None),
            P(("groups", "rhs"), None),
        ),
        out_specs=(P("rhs", ("groups", "space"), None), P("rhs", ("groups", "space"), None)),
        check_vma=False,
    )
```

time: 24.9 us -> 21.9 us (0.88)
  Pallas kernels: 24.1 us -> 21.1 us
    pallas_call x1, Pallas kernels: 21 us -> 18 us  [on_device(): pl.pallas_call(functools.partial(krylov_kernel, count), out_shape=[field]...]
where the time goes in v1:
time: 21.9 us; the launch traced here: 21.7 us
  Pallas kernels  21.1 us (96%)
  between operations  0.64 us (3%)
    pallas_call x1, Pallas kernels, on_device(): pl.pallas_call(functools.partial(krylov_kernel, count), out_shape=[field]...  18 us
    pallas_call x1, Pallas kernels, on_device(): pl.pallas_call(combine_kernel, out_shape=[out, out], in_specs=[vm] * 6, o...  3.06 us

profile of v1, /device:TPU:0, one launch (start us, length us, event | category | flops | bytes accessed | tf_op | source)
XLA Modules:
  0.0 21.7 jit_solution(11229878327318900737)
XLA Ops:
  0.6 18.0 %krylov.1 = (f32[8,72,1024]{2,1,0:T(8,128)S(1)}, f32[8,72,1024]{2,1,0:T(8,128)S(1)}, f32[8,72,1024]{2,1,0:T(8,128)S(1)}, f32[8,72,1024]{2,1,0:T(8,128)S(1)}, f32...) custom-call(f32[8,1024]{1,0:T(8,128)} %cond_hbm.1, s32[8,1024]{1,0:T(8,128)} %nodata_hbm.1, s32[8,1024]{1,0:T(8,128)} %gmask_hbm.1, ...), custom_call_target="tpu_custom_call" | custom-call | tf_op jit(solution)/shard_map/krylov/pallas_call | solution.py:475
  18.7 3.1 %combine.1 = (f32[64,8,1024]{2,1,0:T(8,128)}, f32[64,8,1024]{2,1,0:T(8,128)}) custom-call(f32[64,128]{1,0:T(8,128)S(1)} %get-tuple-element.8.coef_ref, f32[8,72,1024]{2,1,0:T(8,128)S(1)} %get-tuple-element.9.r0_ref, f32[8,72,1024]{2,1,0:T(8,128)S(1)} %get-tuple-element.10.q_ref, f32[8,72,1024]{2,1,0:T(8,128)S(1)} %get-tuple-element.11.w_ref, ...), custom_call_target="tpu_custom_call" | custom-call | tf_op jit(solution)/shard_map/combine/pallas_call | solution.py:514

commit v2 on v1

--- a/solution.py
+++ b/solution.py
@@ -53,10 +53,11 @@
     ]
     for load in loads:
         load.start()
-    for load in loads:
-        load.wait()
+    loads[0].wait()
     for load in t_loads:
         load.start()
+    for load in loads[1:]:
+        load.wait()
 
     def gather(src, at):
         for p in range(pairs):
@@ -413,49 +414,49 @@
     total = early
     for k in range(1, count):
         total = total + all_ref[k - 1]
-    for copy in late_copies:
-        copy.wait()
-    joint = late[0:1, :] + late[1:2, :]
-    for k in range(1, count):
-        joint = joint + jnp.where(k <= me, lates_ref[k - 1, 0:1, :], lates_ref[k - 1, 1:2, :])
     gamma0, kappa, mu, part = (total[i:i + 1, :] for i in range(4))
-    nu = 2.0 * (part - joint)
     a0 = gamma0 / kappa
     gamma1 = a0 * a0 * mu - gamma0
     beta = gamma1 / gamma0
-    a1 = gamma1 / (kappa - 2.0 * a0 * mu + a0 * a0 * nu - beta * gamma1 / a0)
+    known = kappa - 2.0 * a0 * mu - beta * gamma1 / a0 + 2.0 * a0 * a0 * part
+    scale = 2.0 * a0 * a0
+    joint = late[0:1, :] + late[1:2, :]
+    for copy in late_copies:
+        copy.wait()
+    for k in range(1, count):
+        joint = joint + jnp.where(k <= me, lates_ref[k - 1, 0:1, :], lates_ref[k - 1, 1:2, :])
+    a1 = gamma1 / (known - scale * joint)
     first = a0 + a1 * (1.0 + beta)
-    both = jnp.concatenate([first, a0 * a1, jnp.zeros((LANES - 2, LANES), F32)], 0).T
-    coef_ref[...] = jnp.where(lane < LANES // 2, both[:pairs, 0:1], both[:pairs, 1:2])
+    both = jnp.concatenate([first, a0 * a1, jnp.zeros((6, LANES), F32)], 0).T
+    for i in range(2):
+        coef_ref[i] = jnp.broadcast_to(both[:pairs, i:i + 1], (pairs, LANES))
 
 
 def combine_kernel(coef_ref, r0_ref, q_ref, w_ref, z_ref, y_ref, sol_hbm, res_hbm, sol_ref, res_ref, sem):
-    pairs, rows, cols = sol_ref.shape
-    block = 8
-
-    def out(i, src, dst, k):
-        cut = pl.ds(pl.multiple_of(i * block, block), block)
-        return pltpu.make_async_copy(src.at[cut], dst.at[cut], sem.at[k, i])
-
-    def body(i, carry):
-        cut = pl.ds(pl.multiple_of(i * block, block), block)
-        one = coef_ref[cut, 0:1]
-        two = coef_ref[cut, LANES - 1:LANES]
-        for r in range(rows):
-            sol_ref[cut, r, :] = one * q_ref[r, cut, :] - two * z_ref[r, cut, :]
-            res_ref[cut, r, :] = r0_ref[r, cut, :] - one * w_ref[r, cut, :] + two * y_ref[r, cut, :]
-        out(i, sol_ref, sol_hbm, 0).start()
-        out(i, res_ref, res_hbm, 1).start()
+    rows, pairs, cols = sol_ref.shape
+    mine = pl.ds(0, pairs)
+
+    def out(r, src, dst, k):
+        return pltpu.make_async_copy(src.at[r], dst.at[mine, r], sem.at[k, r])
+
+    def body(r, carry):
+        one, two = coef_ref[0], coef_ref[1]
+        for c in range(cols // LANES):
+            cut = slice(c * LANES, (c + 1) * LANES)
+            sol_ref[r, :, cut] = one * q_ref[r, mine, cut] - two * z_ref[r, mine, cut]
+            res_ref[r, :, cut] = r0_ref[r, mine, cut] - one * w_ref[r, mine, cut] + two * y_ref[r, mine, cut]
+        out(r, sol_ref, sol_hbm, 0).start()
+        out(r, res_ref, res_hbm, 1).start()
         return carry
 
-    lax.fori_loop(0, pairs // block, body, 0)
-
-    def finish(i, carry):
-        out(i, sol_ref, sol_hbm, 0).wait()
-        out(i, res_ref, res_hbm, 1).wait()
+    lax.fori_loop(0, rows, body, 0)
+
+    def finish(r, carry):
+        out(r, sol_ref, sol_hbm, 0).wait()
+        out(r, res_ref, res_hbm, 1).wait()
         return carry
 
-    lax.fori_loop(0, pairs // block, finish, 0)
+    lax.fori_loop(0, rows, finish, 0)
 
 
 def on_device(count, cond, nodata, gmask, gval, smask, scur, tinv, focal):
@@ -474,7 +475,7 @@
     small = (rows, cols)
     r0, q, w, z, y, coef = pl.pallas_call(
         functools.partial(krylov_kernel, count),
-        out_shape=[field] * 5 + [jax.ShapeDtypeStruct((pairs, LANES), F32)],
+        out_shape=[field] * 5 + [jax.ShapeDtypeStruct((2, pairs, LANES), F32)],
         in_specs=[hbm] * 8,
         out_specs=[vm] * 6,
         scratch_shapes=[
@@ -517,9 +518,9 @@
         in_specs=[vm] * 6,
         out_specs=[hbm, hbm],
         scratch_shapes=[
-            pltpu.VMEM(out.shape, F32),
-            pltpu.VMEM(out.shape, F32),
-            pltpu.SemaphoreType.DMA((2, pairs // 8)),
+            pltpu.VMEM((rows, pairs, cols), F32),
+            pltpu.VMEM((rows, pairs, cols), F32),
+            pltpu.SemaphoreType.DMA((2, rows)),
         ],
         compiler_params=pltpu.CompilerParams(vmem_limit_bytes=20 * 1024 * 1024),
         name="combine",

time: 21.9 us -> 20.4 us (0.932)
  Pallas kernels: 21.1 us -> 19.6 us
    pallas_call x1, Pallas kernels: 3.06 us -> 2.25 us  [on_device(): pl.pallas_call(combine_kernel, out_shape=[out, out], in_specs=[vm] * 6, o...]
    pallas_call x1, Pallas kernels: 18 us -> 17.3 us  [on_device(): pl.pallas_call(functools.partial(krylov_kernel, count), out_shape=[field]...]
where the time goes in v2:
time: 20.4 us; the launch traced here: 20.2 us
  Pallas kernels  19.6 us (96%)
  between operations  0.64 us (3%)
    pallas_call x1, Pallas kernels, on_device(): pl.pallas_call(functools.partial(krylov_kernel, count), out_shape=[field]...  17.3 us
    pallas_call x1, Pallas kernels, on_device(): pl.pallas_call(combine_kernel, out_shape=[out, out], in_specs=[vm] * 6, o...  2.25 us

profile of v2, /device:TPU:0, one launch (start us, length us, event | category | flops | bytes accessed | tf_op | source)
XLA Modules:
  0.0 20.2 jit_solution(11003365553572083923)
XLA Ops:
  0.6 17.3 %krylov.1 = (f32[8,72,1024]{2,1,0:T(8,128)S(1)}, f32[8,72,1024]{2,1,0:T(8,128)S(1)}, f32[8,72,1024]{2,1,0:T(8,128)S(1)}, f32[8,72,1024]{2,1,0:T(8,128)S(1)}, f32...) custom-call(f32[8,1024]{1,0:T(8,128)} %cond_hbm.1, s32[8,1024]{1,0:T(8,128)} %nodata_hbm.1, s32[8,1024]{1,0:T(8,128)} %gmask_hbm.1, ...), custom_call_target="tpu_custom_call" | custom-call | tf_op jit(solution)/shard_map/krylov/pallas_call | solution.py:476
  18.0 2.3 %combine.1 = (f32[64,8,1024]{2,1,0:T(8,128)}, f32[64,8,1024]{2,1,0:T(8,128)}) custom-call(f32[2,64,128]{2,1,0:T(8,128)S(1)} %get-tuple-element.8.coef_ref, f32[8,72,1024]{2,1,0:T(8,128)S(1)} %get-tuple-element.9.r0_ref, f32[8,72,1024]{2,1,0:T(8,128)S(1)} %get-tuple-element.10.q_ref, f32[8,72,1024]{2,1,0:T(8,128)S(1)} %get-tuple-element.11.w_ref, ...), custom_call_target="tpu_custom_call" | custom-call | tf_op jit(solution)/shard_map/combine/pallas_call | solution.py:515

commit v3 on v2

--- a/solution.py
+++ b/solution.py
@@ -18,12 +18,12 @@
 def krylov_kernel(
     count, cond_hbm, nodata_hbm, gmask_hbm, gval_hbm, smask_hbm, scur_hbm, t_hbm, focal_hbm,
     r0_ref, q_ref, w_ref, z_ref, y_ref, coef_ref,
-    cond_ref, nodata_ref, gmask_ref, gval_ref, smask_ref, scur_ref, focal_ref, ids_ref, te_ref, ti_ref,
+    reals_ref, flags_ref, focal_ref, ids_ref, te_ref, ti_ref,
     thl_ref, wts_ref, spot_ref, qhalo_ref, zhalo_ref, msg_ref, got_ref, bmsg_ref, bgot_ref, tmsg_ref, tgot_ref,
     zmsg_ref, zgot_ref, acc_ref, stat_ref, all_ref, late_ref, lates_ref,
-    send1, recv1, sendb, recvb, sendt, recvt, send2, recv2, send3, recv3, send4, recv4, sem_in, sem_t,
+    send1, recv1, sendb, recvb, sendt, recvt, send2, recv2, send3, recv3, send4, recv4, sem_in,
 ):
-    rows, cols = cond_ref.shape
+    rows, cols = reals_ref.shape[1:]
     tiles = cols // LANES
     pairs = focal_ref.shape[1]
     ext = pairs + EXTRA
@@ -40,34 +40,36 @@
             device_id_type=pl.DeviceIdType.MESH,
         )
 
-    loads = [
-        pltpu.make_async_copy(src, dst, sem_in.at[i])
-        for i, (src, dst) in enumerate((
-            (focal_hbm, ids_ref), (focal_hbm, focal_ref), (t_hbm.at[0], te_ref.at[pl.ds(0, cols)]),
-            (t_hbm.at[rows - 1], te_ref.at[pl.ds(cols, cols)]), (smask_hbm, smask_ref), (scur_hbm, scur_ref),
-            (cond_hbm, cond_ref), (nodata_hbm, nodata_ref), (gmask_hbm, gmask_ref), (gval_hbm, gval_ref),
-        ))
-    ]
-    t_loads = [
-        pltpu.make_async_copy(t_hbm.at[r], ti_ref.at[pl.ds((r - 1) * cols, cols)], sem_t.at[r]) for r in inner
-    ]
-    for load in loads:
-        load.start()
-    loads[0].wait()
-    for load in t_loads:
-        load.start()
-    for load in loads[1:]:
-        load.wait()
+    def whole(ref, i):
+        return pltpu.make_async_copy(ref, ref, sem_in.at[i])
+
+    ids_load = pltpu.make_async_copy(focal_hbm, ids_ref, sem_in.at[0])
+    focal_load = pltpu.make_async_copy(focal_hbm, focal_ref, sem_in.at[1])
+    inner_load = pltpu.make_async_copy(t_hbm.at[pl.ds(1, rows - 2)], ti_ref, sem_in.at[5])
+    ids_load.start()
+    focal_load.start()
+    for side, r in ends:
+        for cut in cuts:
+            pltpu.make_async_copy(
+                t_hbm.at[r, pl.ds(cut.start, LANES)], te_ref.at[side, pl.ds(cut.start, LANES)], sem_in.at[2]).start()
+    for i, group in ((3, (cond_hbm, gval_hbm, scur_hbm)), (4, (nodata_hbm, gmask_hbm, smask_hbm))):
+        for k, src in enumerate(group):
+            pltpu.make_async_copy(src, (reals_ref, flags_ref)[i - 3].at[k], sem_in.at[i]).start()
+    inner_load.start()
+    ids_load.wait()
+    focal_load.wait()
+    whole(te_ref, 2).wait()
 
     def gather(src, at):
         for p in range(pairs):
             for i in range(2):
-                spot_ref[i, p:p + 1, :] = src[pl.ds(at(ids_ref[i, p]), 1), :]
+                r, k = at(ids_ref[i, p])
+                spot_ref[i, p:p + 1, :] = src[r, pl.ds(k, 1), :]
         return FOCAL_CURRENT * spot_ref[0], -FOCAL_CURRENT * spot_ref[1]
 
-    half = (rows * cols // 2).bit_length() - 1
+    half, high = (rows * cols // 2).bit_length() - 1, cols.bit_length() - 1
     near_a, near_b = gather(
-        te_ref, lambda i: (i & (cols - 1)) + (lax.shift_right_logical(i, half) & 1) * cols)
+        te_ref, lambda i: (lax.shift_right_logical(i, half) & 1, i & (cols - 1)))
 
     diagonal = lax.broadcasted_iota(jnp.int32, (pairs, pairs), 0) == lax.broadcasted_iota(
         jnp.int32, (pairs, pairs), 1)
@@ -124,14 +126,16 @@
     pl.semaphore_wait(barrier, last)
     send(msg_ref, got_ref, send1, recv1)
 
-    valid = (1 - nodata_ref[...]).astype(F32)
-    active = cond_ref[...] * valid
-    background = smask_ref[...].astype(F32) * scur_ref[...]
+    whole(reals_ref, 3).wait()
+    whole(flags_ref, 4).wait()
+    valid = (1 - flags_ref[0]).astype(F32)
+    active = reals_ref[0] * valid
+    background = flags_ref[2].astype(F32) * reals_ref[2]
 
     def tile_of(r, c):
         if r == 0 or r == rows - 1:
-            return te_ref[pl.ds((cols if r else 0) + c * LANES, LANES), :]
-        return ti_ref[pl.ds((r - 1) * cols + c * LANES, LANES), :]
+            return te_ref[min(r, 1), cuts[c], :]
+        return ti_ref[r - 1, cuts[c], :]
 
     def product(x, r, c):
         number = x.shape[0]
@@ -159,10 +163,8 @@
             bmsg_ref[side, c:c + 1, :] = q_ref[r, pairs:pairs + 1, cut]
             bmsg_ref[side, tiles + c:tiles + c + 1, :] = active[r:r + 1, cut]
             bmsg_ref[side, 2 * tiles + c:2 * tiles + c + 1, :] = valid[r:r + 1, cut]
-            first = r and cols
-            tmsg_ref[side, c:c + 1, :] = te_ref[first + c * LANES:first + c * LANES + 1, :]
-            tmsg_ref[side, tiles + c:tiles + c + 1, :] = te_ref[
-                first + c * LANES + LANES - 1:first + (c + 1) * LANES, :]
+            tmsg_ref[side, c:c + 1, :] = te_ref[side, cut.start:cut.start + 1, :]
+            tmsg_ref[side, tiles + c:tiles + c + 1, :] = te_ref[side, cut.stop - 1:cut.stop, :]
     send(bmsg_ref, bgot_ref, sendb, recvb)
     send(tmsg_ref, tgot_ref, sendt, recvt)
 
@@ -181,15 +183,15 @@
         edge(active, shifted(active, *how), valid, shifted(valid, *how))
         for how in ((1, 0), (-1, 0), (1, 1), (-1, 1))
     )
-    dg = valid * (LEAKAGE + gmask_ref[...].astype(F32) * gval_ref[...]) + (1.0 - valid) + nw + sw + ww + ew
+    dg = valid * (LEAKAGE + flags_ref[1].astype(F32) * reals_ref[1]) + (1.0 - valid) + nw + sw + ww + ew
     for r in range(rows):
         for i, x in enumerate((dg, nw, sw, ww, ew, 0.5 * dg, background)):
             wts_ref[r, i:i + 1, :] = x[r:r + 1, :]
 
-    for load in t_loads:
-        load.wait()
+    inner_load.wait()
     far_a, far_b = gather(
-        ti_ref, lambda i: jnp.clip((i & (rows * cols - 1)) - cols, 0, (rows - 2) * cols - 1))
+        ti_ref, lambda i: (
+            jnp.clip((lax.shift_right_logical(i, high) & (rows - 1)) - 1, 0, rows - 3), i & (cols - 1)))
     for r in inner:
         shared = shared + shared_row(r)
 
@@ -216,31 +218,35 @@
     for i in range(1, 4):
         acc_ref[i] = jnp.zeros(acc_ref.shape[1:], F32)
 
-    parts = [slice(p, p + pairs // 2) for p in (0, pairs // 2)]
+    parts = [slice(p, p + 16) for p in range(0, pairs, 16)]
     extra = slice(pairs, ext)
 
-    def sides(xs):
-        at = lane[:xs[0].shape[0]]
-        west = [pltpu.roll(x, 1, 1) for x in xs]
-        east = [pltpu.roll(x, LANES - 1, 1) for x in xs]
-        west = west[:1] + [jnp.where(at == 0, west[c - 1], west[c]) for c in range(1, tiles)]
-        east = [jnp.where(at == LANES - 1, east[c + 1], east[c]) for c in range(tiles - 1)] + east[-1:]
-        return west, east
+    def stream(src, r, s, east=True):
+        at = lane[:s.stop - s.start]
+        x = src[r, s, cuts[0]]
+        gone, west, ahead = None, pltpu.roll(x, 1, 1), east and pltpu.roll(x, LANES - 1, 1)
+        for c in range(tiles):
+            more = c + 1 < tiles
+            if more:
+                y = src[r, s, cuts[c + 1]]
+                after = east and pltpu.roll(y, LANES - 1, 1)
+            yield (
+                c, cuts[c], x, west if gone is None else jnp.where(at == 0, gone, west),
+                jnp.where(at == LANES - 1, after, ahead) if east and more else ahead,
+            )
+            if more:
+                x, gone, west, ahead = y, west, pltpu.roll(y, 1, 1), after
 
     def apply_part(src, dst, r, s, north, south, acc=None):
-        xs = [src[r, s, cut] for cut in cuts]
-        west, east = sides(xs)
         dots = None
-        for c, cut in enumerate(cuts):
-            out = (
-                wts_ref[r, 0:1, cut] * xs[c] - wts_ref[r, 3:4, cut] * west[c] - wts_ref[r, 4:5, cut] * east[c]
-            )
+        for c, cut, x, west, east in stream(src, r, s):
+            out = wts_ref[r, 0:1, cut] * x - wts_ref[r, 3:4, cut] * west - wts_ref[r, 4:5, cut] * east
             if north is not None:
                 out = out - wts_ref[r, 1:2, cut] * north[0][north[1], s, cut]
             if south is not None:
                 out = out - wts_ref[r, 2:3, cut] * south[0][south[1], s, cut]
             dst[r, s, cut] = out
-            dots = xs[c] * out if dots is None else dots + xs[c] * out
+            dots = x * out if dots is None else dots + x * out
         if acc is not None:
             acc_ref[acc, s, :] += dots
 
@@ -253,7 +259,6 @@
             return carry
         lax.fori_loop(1, rows - 1, body, 0)
 
-    apply_inner(q_ref, w_ref, True, 1)
     for s in (*parts, extra):
         apply_part(q_ref, w_ref, 0, s, None, (q_ref, 1))
         apply_part(q_ref, w_ref, rows - 1, s, (q_ref, rows - 2), None)
@@ -308,18 +313,17 @@
         pack(z_ref, r, zmsg_ref, side)
     send(zmsg_ref, zgot_ref, send2, recv2)
 
+    apply_inner(q_ref, w_ref, True, 1)
     for r in inner:
         precond_row(r)
 
     def moment_part(r, s, north):
-        zs = [z_ref[r, s, cut] for cut in cuts]
-        west, _ = sides(zs)
         mu = nu = None
-        for c, cut in enumerate(cuts):
-            t = wts_ref[r, 5:6, cut] * zs[c] - wts_ref[r, 3:4, cut] * west[c]
+        for c, cut, z, west, _ in stream(z_ref, r, s, False):
+            t = wts_ref[r, 5:6, cut] * z - wts_ref[r, 3:4, cut] * west
             if north:
                 t = t - wts_ref[r, 1:2, cut] * z_ref[r - 1, s, cut]
-            one, two = w_ref[r, s, cut] * zs[c], t * zs[c]
+            one, two = w_ref[r, s, cut] * z, t * z
             mu, nu = (one, two) if mu is None else (mu + one, nu + two)
         acc_ref[2, s, :] += mu
         acc_ref[3, s, :] += nu
@@ -333,31 +337,28 @@
         moment_part(0, s, False)
     lax.fori_loop(1, rows, moments, 0)
 
-    square = lax.broadcasted_iota(jnp.int32, (LANES, LANES), 1)
-    pad = jnp.zeros((LANES - pairs, 1), F32)
+    pad = jnp.zeros((8, LANES - pairs), F32)
 
     def lines(sums):
-        table = jnp.zeros((LANES, LANES), F32)
+        table = jnp.zeros((pairs, LANES), F32)
         for i, x in enumerate(sums):
-            col = jnp.concatenate([jnp.sum(x, 1, keepdims=True), pad], 0)
-            table = jnp.where(square == i, jnp.broadcast_to(col, table.shape), table)
-        return table.T[0:8, :]
+            table = jnp.where(lane == i, jnp.sum(x, 1, keepdims=True), table)
+        return jnp.concatenate([table.T[0:8, :], pad], 1)
 
     def exchange(src, dst, ssem, rsem):
-        return [
+        for k in range(1, count):
             pltpu.make_async_remote_copy(
-                src_ref=src, dst_ref=dst.at[k - 1],
-                send_sem=ssem.at[k - 1], recv_sem=rsem.at[k - 1],
+                src_ref=src, dst_ref=dst.at[k - 1], send_sem=ssem, recv_sem=rsem,
                 device_id={"space": lax.rem(me + k, count)}, device_id_type=pl.DeviceIdType.MESH,
-            )
-            for k in range(1, count)
-        ]
+            ).start()
+
+    def arrived(dst, ssem, rsem):
+        for sem in (ssem, rsem):
+            pltpu.make_async_copy(dst, dst, sem).wait()
 
     early = lines([acc_ref[i] for i in range(4)])
     stat_ref[...] = early
-    early_copies = exchange(stat_ref, all_ref, send3, recv3)
-    for copy in early_copies:
-        copy.start()
+    exchange(stat_ref, all_ref, send3, recv3)
 
     done(tmsg_ref, tgot_ref, sendt, recvt)
     for side in range(2):
@@ -391,9 +392,7 @@
         coupling.append(total)
     late = lines(coupling)
     late_ref[...] = late
-    late_copies = exchange(late_ref, lates_ref, send4, recv4)
-    for copy in late_copies:
-        copy.start()
+    exchange(late_ref, lates_ref, send4, recv4)
 
     apply_inner(z_ref, y_ref, False)
     for s in parts:
@@ -409,8 +408,7 @@
 
     lax.fori_loop(0, rows, right_side, 0)
 
-    for copy in early_copies:
-        copy.wait()
+    arrived(all_ref, send3, recv3)
     total = early
     for k in range(1, count):
         total = total + all_ref[k - 1]
@@ -421,8 +419,7 @@
     known = kappa - 2.0 * a0 * mu - beta * gamma1 / a0 + 2.0 * a0 * a0 * part
     scale = 2.0 * a0 * a0
     joint = late[0:1, :] + late[1:2, :]
-    for copy in late_copies:
-        copy.wait()
+    arrived(lates_ref, send4, recv4)
     for k in range(1, count):
         joint = joint + jnp.where(k <= me, lates_ref[k - 1, 0:1, :], lates_ref[k - 1, 1:2, :])
     a1 = gamma1 / (known - scale * joint)
@@ -472,23 +469,18 @@
     tmsg = (2, 2 * tiles, LANES)
     zmsg = (2, 2 * pairs + tiles, LANES)
     others = count - 1
-    small = (rows, cols)
     r0, q, w, z, y, coef = pl.pallas_call(
         functools.partial(krylov_kernel, count),
         out_shape=[field] * 5 + [jax.ShapeDtypeStruct((2, pairs, LANES), F32)],
         in_specs=[hbm] * 8,
         out_specs=[vm] * 6,
         scratch_shapes=[
-            pltpu.VMEM(small, F32),
-            pltpu.VMEM(small, jnp.int32),
-            pltpu.VMEM(small, jnp.int32),
-            pltpu.VMEM(small, F32),
-            pltpu.VMEM(small, jnp.int32),
-            pltpu.VMEM(small, F32),
+            pltpu.VMEM((3, rows, cols), F32),
+            pltpu.VMEM((3, rows, cols), jnp.int32),
             pltpu.VMEM((2, pairs), jnp.int32),
             pltpu.SMEM((2, pairs), jnp.int32),
-            pltpu.VMEM((2 * cols, LANES), F32),
-            pltpu.VMEM(((rows - 2) * cols, LANES), F32),
+            pltpu.VMEM((2, cols, LANES), F32),
+            pltpu.VMEM((rows - 2, cols, LANES), F32),
             pltpu.VMEM((rows, tiles, LANES, 2 * LANES), BF16),
             pltpu.VMEM((rows, 8, cols), F32),
             pltpu.VMEM((2, pairs, LANES), F32),
@@ -498,9 +490,8 @@
             pltpu.VMEM((4, pairs, LANES), F32),
             *[pltpu.VMEM(shape, F32) for _ in range(2) for shape in ((8, LANES), (others, 8, LANES))],
             *[pltpu.SemaphoreType.DMA((2,))] * 8,
-            *[pltpu.SemaphoreType.DMA((others,))] * 4,
-            pltpu.SemaphoreType.DMA((10,)),
-            pltpu.SemaphoreType.DMA((rows,)),
+            *[pltpu.SemaphoreType.DMA] * 4,
+            pltpu.SemaphoreType.DMA((6,)),
         ],
         compiler_params=pltpu.CompilerParams(
             collective_id=0, has_side_effects=True, vmem_limit_bytes=36 * 1024 * 1024

time: 20.4 us -> 19.7 us (0.966)
  Pallas kernels: 19.6 us -> 18.9 us
    pallas_call x1, Pallas kernels: 17.3 us -> 16.6 us  [on_device(): pl.pallas_call(functools.partial(krylov_kernel, count), out_shape=[field]...]
where the time goes in v3:
time: 19.7 us; the launch traced here: 19.5 us
  Pallas kernels  18.9 us (96%)
  between operations  0.64 us (3%)
    pallas_call x1, Pallas kernels, on_device(): pl.pallas_call(functools.partial(krylov_kernel, count), out_shape=[field]...  16.6 us
    pallas_call x1, Pallas kernels, on_device(): pl.pallas_call(combine_kernel, out_shape=[out, out], in_specs=[vm] * 6, o...  2.25 us

profile of v3, /device:TPU:0, one launch (start us, length us, event | category | flops | bytes accessed | tf_op | source)
XLA Modules:
  0.0 19.5 jit_solution(9903086297400362815)
XLA Ops:
  0.6 16.6 %krylov.1 = (f32[8,72,1024]{2,1,0:T(8,128)S(1)}, f32[8,72,1024]{2,1,0:T(8,128)S(1)}, f32[8,72,1024]{2,1,0:T(8,128)S(1)}, f32[8,72,1024]{2,1,0:T(8,128)S(1)}, f32...) custom-call(f32[8,1024]{1,0:T(8,128)} %cond_hbm.1, s32[8,1024]{1,0:T(8,128)} %nodata_hbm.1, s32[8,1024]{1,0:T(8,128)} %gmask_hbm.1, ...), custom_call_target="tpu_custom_call" | custom-call | tf_op jit(solution)/shard_map/krylov/pallas_call | solution.py:472
  17.3 2.3 %combine.1 = (f32[64,8,1024]{2,1,0:T(8,128)}, f32[64,8,1024]{2,1,0:T(8,128)}) custom-call(f32[2,64,128]{2,1,0:T(8,128)S(1)} %get-tuple-element.8.coef_ref, f32[8,72,1024]{2,1,0:T(8,128)S(1)} %get-tuple-element.9.r0_ref, f32[8,72,1024]{2,1,0:T(8,128)S(1)} %get-tuple-element.10.q_ref, f32[8,72,1024]{2,1,0:T(8,128)S(1)} %get-tuple-element.11.w_ref, ...), custom_call_target="tpu_custom_call" | custom-call | tf_op jit(solution)/shard_map/combine/pallas_call | solution.py:506

commit v4 on v3

--- a/solution.py
+++ b/solution.py
@@ -21,7 +21,7 @@
     reals_ref, flags_ref, focal_ref, ids_ref, te_ref, ti_ref,
     thl_ref, wts_ref, spot_ref, qhalo_ref, zhalo_ref, msg_ref, got_ref, bmsg_ref, bgot_ref, tmsg_ref, tgot_ref,
     zmsg_ref, zgot_ref, acc_ref, stat_ref, all_ref, late_ref, lates_ref,
-    send1, recv1, sendb, recvb, sendt, recvt, send2, recv2, send3, recv3, send4, recv4, sem_in,
+    send1, recv1, sendb, recvb, sendt, recvt, send2, recv2, send3, recv3, send4, recv4, sem_in, hello,
 ):
     rows, cols = reals_ref.shape[1:]
     tiles = cols // LANES
@@ -33,12 +33,30 @@
     inner = range(1, rows - 1)
     cuts = [slice(c * LANES, (c + 1) * LANES) for c in range(tiles)]
 
+    has = (me > 0, me < last)
+    few = count <= 4
     barrier = pltpu.get_barrier_semaphore()
-    for off in range(1, count):
-        pl.semaphore_signal(
-            barrier, inc=1, device_id={"space": lax.rem(me + off, count)},
-            device_id_type=pl.DeviceIdType.MESH,
-        )
+
+    def greet(sem):
+        for side in range(2):
+            @pl.when(has[side])
+            def _():
+                pl.semaphore_signal(
+                    sem, inc=1, device_id={"space": me - 1 if side == 0 else me + 1},
+                    device_id_type=pl.DeviceIdType.MESH,
+                )
+
+    def greeted(sem):
+        pl.semaphore_wait(sem, jnp.minimum(me, 1) + jnp.minimum(last - me, 1))
+
+    if few:
+        greet(barrier)
+    else:
+        for off in range(1, count):
+            pl.semaphore_signal(
+                barrier, inc=1, device_id={"space": lax.rem(me + off, count)},
+                device_id_type=pl.DeviceIdType.MESH,
+            )
 
     def whole(ref, i):
         return pltpu.make_async_copy(ref, ref, sem_in.at[i])
@@ -99,8 +117,6 @@
             device_id_type=pl.DeviceIdType.MESH,
         )
 
-    has = (me > 0, me < last)
-
     def send(src, dst, ssem, rsem):
         for side in range(2):
             @pl.when(has[side])
@@ -123,7 +139,10 @@
                     device_id_type=pl.DeviceIdType.MESH,
                 ).wait_recv()
 
-    pl.semaphore_wait(barrier, last)
+    if few:
+        greeted(barrier)
+    else:
+        pl.semaphore_wait(barrier, last)
     send(msg_ref, got_ref, send1, recv1)
 
     whole(reals_ref, 3).wait()
@@ -264,6 +283,8 @@
         apply_part(q_ref, w_ref, rows - 1, s, (q_ref, rows - 2), None)
 
     done(msg_ref, got_ref, send1, recv1)
+    if few:
+        greet(hello)
     done(bmsg_ref, bgot_ref, sendb, recvb)
 
     def row_of(side, base):
@@ -358,6 +379,8 @@
 
     early = lines([acc_ref[i] for i in range(4)])
     stat_ref[...] = early
+    if few:
+        greeted(hello)
     exchange(stat_ref, all_ref, send3, recv3)
 
     done(tmsg_ref, tgot_ref, sendt, recvt)
@@ -492,6 +515,7 @@
             *[pltpu.SemaphoreType.DMA((2,))] * 8,
             *[pltpu.SemaphoreType.DMA] * 4,
             pltpu.SemaphoreType.DMA((6,)),
+            pltpu.SemaphoreType.REGULAR,
         ],
         compiler_params=pltpu.CompilerParams(
             collective_id=0, has_side_effects=True, vmem_limit_bytes=36 * 1024 * 1024

time: 19.7 us -> 19.7 us (level)
  no operation moved by 1% of the time
where the time goes in v4:
time: 19.7 us; the launch traced here: 19.5 us
  Pallas kernels  18.9 us (96%)
  between operations  0.64 us (3%)
    pallas_call x1, Pallas kernels, on_device(): pl.pallas_call(functools.partial(krylov_kernel, count), out_shape=[field]...  16.6 us
    pallas_call x1, Pallas kernels, on_device(): pl.pallas_call(combine_kernel, out_shape=[out, out], in_specs=[vm] * 6, o...  2.25 us

profile of v4, /device:TPU:0, one launch (start us, length us, event | category | flops | bytes accessed | tf_op | source)
XLA Modules:
  0.0 19.5 jit_solution(8681651578702098458)
XLA Ops:
  0.6 16.6 %krylov.1 = (f32[8,72,1024]{2,1,0:T(8,128)S(1)}, f32[8,72,1024]{2,1,0:T(8,128)S(1)}, f32[8,72,1024]{2,1,0:T(8,128)S(1)}, f32[8,72,1024]{2,1,0:T(8,128)S(1)}, f32...) custom-call(f32[8,1024]{1,0:T(8,128)} %cond_hbm.1, s32[8,1024]{1,0:T(8,128)} %nodata_hbm.1, s32[8,1024]{1,0:T(8,128)} %gmask_hbm.1, ...), custom_call_target="tpu_custom_call" | custom-call | tf_op jit(solution)/shard_map/krylov/pallas_call | solution.py:495
  17.3 2.3 %combine.1 = (f32[64,8,1024]{2,1,0:T(8,128)}, f32[64,8,1024]{2,1,0:T(8,128)}) custom-call(f32[2,64,128]{2,1,0:T(8,128)S(1)} %get-tuple-element.8.coef_ref, f32[8,72,1024]{2,1,0:T(8,128)S(1)} %get-tuple-element.9.r0_ref, f32[8,72,1024]{2,1,0:T(8,128)S(1)} %get-tuple-element.10.q_ref, f32[8,72,1024]{2,1,0:T(8,128)S(1)} %get-tuple-element.11.w_ref, ...), custom_call_target="tpu_custom_call" | custom-call | tf_op jit(solution)/shard_map/combine/pallas_call | solution.py:530

commit v5 on v4

--- a/solution.py
+++ b/solution.py
@@ -269,12 +269,10 @@
         if acc is not None:
             acc_ref[acc, s, :] += dots
 
-    def apply_inner(src, dst, both, acc=None):
+    def apply_inner(src, dst):
         def body(r, carry):
             for s in parts:
-                apply_part(src, dst, r, s, (src, r - 1), (src, r + 1), acc)
-            if both:
-                apply_part(src, dst, r, extra, (src, r - 1), (src, r + 1))
+                apply_part(src, dst, r, s, (src, r - 1), (src, r + 1))
             return carry
         lax.fori_loop(1, rows - 1, body, 0)
 
@@ -334,9 +332,6 @@
         pack(z_ref, r, zmsg_ref, side)
     send(zmsg_ref, zgot_ref, send2, recv2)
 
-    apply_inner(q_ref, w_ref, True, 1)
-    for r in inner:
-        precond_row(r)
 
     def moment_part(r, s, north):
         mu = nu = None
@@ -349,14 +344,23 @@
         acc_ref[2, s, :] += mu
         acc_ref[3, s, :] += nu
 
-    def moments(r, carry):
+    def image_row(r):
         for s in parts:
-            moment_part(r, s, True)
-        return carry
-
-    for s in parts:
-        moment_part(0, s, False)
-    lax.fori_loop(1, rows, moments, 0)
+            apply_part(q_ref, w_ref, r, s, (q_ref, r - 1), (q_ref, r + 1), 1)
+        apply_part(q_ref, w_ref, r, extra, (q_ref, r - 1), (q_ref, r + 1))
+
+    def moment_row(r):
+        for s in parts:
+            moment_part(r, s, r > 0)
+
+    image_row(1)
+    for r in inner:
+        if r + 1 in inner:
+            image_row(r + 1)
+        precond_row(r)
+        moment_row(r - 1)
+    moment_row(rows - 2)
+    moment_row(rows - 1)
 
     pad = jnp.zeros((8, LANES - pairs), F32)
 
@@ -417,7 +421,7 @@
     late_ref[...] = late
     exchange(late_ref, lates_ref, send4, recv4)
 
-    apply_inner(z_ref, y_ref, False)
+    apply_inner(z_ref, y_ref)
     for s in parts:
         apply_part(z_ref, y_ref, 0, s, (zhalo_ref, 0), (z_ref, 1))
         apply_part(z_ref, y_ref, rows - 1, s, (z_ref, rows - 2), (zhalo_ref, 1))

time: 19.7 us -> 19.3 us (0.980)
  Pallas kernels: 18.9 us -> 18.5 us
    pallas_call x1, Pallas kernels: 16.6 us -> 16.2 us  [on_device(): pl.pallas_call(functools.partial(krylov_kernel, count), out_shape=[field]...]
where the time goes in v5:
time: 19.3 us; the launch traced here: 19.1 us
  Pallas kernels  18.5 us (96%)
  between operations  0.64 us (3%)
    pallas_call x1, Pallas kernels, on_device(): pl.pallas_call(functools.partial(krylov_kernel, count), out_shape=[field]...  16.2 us
    pallas_call x1, Pallas kernels, on_device(): pl.pallas_call(combine_kernel, out_shape=[out, out], in_specs=[vm] * 6, o...  2.25 us

profile of v5, /device:TPU:0, one launch (start us, length us, event | category | flops | bytes accessed | tf_op | source)
XLA Modules:
  0.0 19.1 jit_solution(9463954496261868762)
XLA Ops:
  0.6 16.2 %krylov.1 = (f32[8,72,1024]{2,1,0:T(8,128)S(1)}, f32[8,72,1024]{2,1,0:T(8,128)S(1)}, f32[8,72,1024]{2,1,0:T(8,128)S(1)}, f32[8,72,1024]{2,1,0:T(8,128)S(1)}, f32...) custom-call(f32[8,1024]{1,0:T(8,128)} %cond_hbm.1, s32[8,1024]{1,0:T(8,128)} %nodata_hbm.1, s32[8,1024]{1,0:T(8,128)} %gmask_hbm.1, ...), custom_call_target="tpu_custom_call" | custom-call | tf_op jit(solution)/shard_map/krylov/pallas_call | solution.py:499
  16.9 2.3 %combine.1 = (f32[64,8,1024]{2,1,0:T(8,128)}, f32[64,8,1024]{2,1,0:T(8,128)}) custom-call(f32[2,64,128]{2,1,0:T(8,128)S(1)} %get-tuple-element.8.coef_ref, f32[8,72,1024]{2,1,0:T(8,128)S(1)} %get-tuple-element.9.r0_ref, f32[8,72,1024]{2,1,0:T(8,128)S(1)} %get-tuple-element.10.q_ref, f32[8,72,1024]{2,1,0:T(8,128)S(1)} %get-tuple-element.11.w_ref, ...), custom_call_target="tpu_custom_call" | custom-call | tf_op jit(solution)/shard_map/combine/pallas_call | solution.py:534

commit v6 on v5

--- a/solution.py
+++ b/solution.py
@@ -36,6 +36,7 @@
     has = (me > 0, me < last)
     few = count <= 4
     barrier = pltpu.get_barrier_semaphore()
+    lates_ref[...] = jnp.zeros(lates_ref.shape, F32)
 
     def greet(sem):
         for side in range(2):
@@ -419,7 +420,20 @@
         coupling.append(total)
     late = lines(coupling)
     late_ref[...] = late
-    exchange(late_ref, lates_ref, send4, recv4)
+    def late_copy(k):
+        return pltpu.make_async_remote_copy(
+            src_ref=late_ref, dst_ref=lates_ref.at[k - 1], send_sem=send4.at[k - 1], recv_sem=recv4.at[k - 1],
+            device_id={"space": lax.rem(me + k, count)}, device_id_type=pl.DeviceIdType.MESH,
+        )
+
+    def gives(who, k):
+        up = who + k < count
+        return jnp.logical_or(jnp.logical_and(up, who > 0), jnp.logical_and(jnp.logical_not(up), who < last))
+
+    for k in range(1, count):
+        @pl.when(gives(me, k))
+        def _():
+            late_copy(k).start()
 
     apply_inner(z_ref, y_ref)
     for s in parts:
@@ -446,7 +460,14 @@
     known = kappa - 2.0 * a0 * mu - beta * gamma1 / a0 + 2.0 * a0 * a0 * part
     scale = 2.0 * a0 * a0
     joint = late[0:1, :] + late[1:2, :]
-    arrived(lates_ref, send4, recv4)
+    for k in range(1, count):
+        @pl.when(gives(me, k))
+        def _():
+            late_copy(k).wait_send()
+
+        @pl.when(gives(lax.rem(me - k + count, count), k))
+        def _():
+            late_copy(k).wait_recv()
     for k in range(1, count):
         joint = joint + jnp.where(k <= me, lates_ref[k - 1, 0:1, :], lates_ref[k - 1, 1:2, :])
     a1 = gamma1 / (known - scale * joint)
@@ -517,7 +538,8 @@
             pltpu.VMEM((4, pairs, LANES), F32),
             *[pltpu.VMEM(shape, F32) for _ in range(2) for shape in ((8, LANES), (others, 8, LANES))],
             *[pltpu.SemaphoreType.DMA((2,))] * 8,
-            *[pltpu.SemaphoreType.DMA] * 4,
+            *[pltpu.SemaphoreType.DMA] * 2,
+            *[pltpu.SemaphoreType.DMA((others,))] * 2,
             pltpu.SemaphoreType.DMA((6,)),
             pltpu.SemaphoreType.REGULAR,
         ],

time: 19.3 us -> 18.6 us (0.964)
  Pallas kernels: 18.5 us -> 17.8 us
    pallas_call x1, Pallas kernels: 16.2 us -> 15.6 us  [on_device(): pl.pallas_call(functools.partial(krylov_kernel, count), out_shape=[field]...]
where the time goes in v6:
time: 18.6 us; the launch traced here: 18.5 us
  Pallas kernels  17.8 us (96%)
  between operations  0.64 us (3%)
    pallas_call x1, Pallas kernels, on_device(): pl.pallas_call(functools.partial(krylov_kernel, count), out_shape=[field]...  15.6 us
    pallas_call x1, Pallas kernels, on_device(): pl.pallas_call(combine_kernel, out_shape=[out, out], in_specs=[vm] * 6, o...  2.25 us

profile of v6, /device:TPU:0, one launch (start us, length us, event | category | flops | bytes accessed | tf_op | source)
XLA Modules:
  0.0 18.5 jit_solution(13585841890113783438)
XLA Ops:
  0.6 15.6 %krylov.1 = (f32[8,72,1024]{2,1,0:T(8,128)S(1)}, f32[8,72,1024]{2,1,0:T(8,128)S(1)}, f32[8,72,1024]{2,1,0:T(8,128)S(1)}, f32[8,72,1024]{2,1,0:T(8,128)S(1)}, f32...) custom-call(f32[8,1024]{1,0:T(8,128)} %cond_hbm.1, s32[8,1024]{1,0:T(8,128)} %nodata_hbm.1, s32[8,1024]{1,0:T(8,128)} %gmask_hbm.1, ...), custom_call_target="tpu_custom_call" | custom-call | tf_op jit(solution)/shard_map/krylov/pallas_call | solution.py:520
  16.2 2.3 %combine.1 = (f32[64,8,1024]{2,1,0:T(8,128)}, f32[64,8,1024]{2,1,0:T(8,128)}) custom-call(f32[2,64,128]{2,1,0:T(8,128)S(1)} %get-tuple-element.8.coef_ref, f32[8,72,1024]{2,1,0:T(8,128)S(1)} %get-tuple-element.9.r0_ref, f32[8,72,1024]{2,1,0:T(8,128)S(1)} %get-tuple-element.10.q_ref, f32[8,72,1024]{2,1,0:T(8,128)S(1)} %get-tuple-element.11.w_ref, ...), custom_call_target="tpu_custom_call" | custom-call | tf_op jit(solution)/shard_map/combine/pallas_call | solution.py:556

commit v7 on v6

--- a/solution.py
+++ b/solution.py
@@ -106,45 +106,58 @@
     def within(spot, low, high):
         return jnp.logical_and(spot >= low * tiles, spot < high * tiles)
 
+    piece = pairs // 2
+    halves = tuple(enumerate((slice(0, piece), slice(piece, pairs))))
     for side, r in ends:
-        msg_ref[side, 0:pairs, :] = jnp.where(within(spot_a, r, r + 1), near_a, 0.0)
-        msg_ref[side, pairs:2 * pairs, :] = jnp.where(within(spot_b, r, r + 1), near_b, 0.0)
-
-    def side_copy(src, dst, ssem, rsem, side):
+        here_a = jnp.where(within(spot_a, r, r + 1), near_a, 0.0)
+        here_b = jnp.where(within(spot_b, r, r + 1), near_b, 0.0)
+        for h, s in halves:
+            msg_ref[h, side, 0:piece, :] = here_a[s]
+            msg_ref[h, side, piece:pairs, :] = here_b[s]
+
+    def side_copy(src, dst, ssem, rsem, side, number):
         return pltpu.make_async_remote_copy(
-            src_ref=src.at[side], dst_ref=dst.at[1 - side],
+            src_ref=src.at[side, pl.ds(0, number)], dst_ref=dst.at[1 - side, pl.ds(0, number)],
             send_sem=ssem.at[side], recv_sem=rsem.at[1 - side],
             device_id={"space": me - 1 if side == 0 else me + 1},
             device_id_type=pl.DeviceIdType.MESH,
         )
 
-    def send(src, dst, ssem, rsem):
+    def send(src, dst, ssem, rsem, number=None):
+        number = number or src.shape[1]
         for side in range(2):
             @pl.when(has[side])
             def _():
-                side_copy(src, dst, ssem, rsem, side).start()
+                side_copy(src, dst, ssem, rsem, side, number).start()
 
             @pl.when(jnp.logical_not(has[side]))
             def _():
                 dst[side] = jnp.zeros(dst.shape[1:], F32)
 
-    def done(src, dst, ssem, rsem):
+    def done(src, dst, ssem, rsem, number=None):
+        number = number or src.shape[1]
         for side in range(2):
             @pl.when(has[side])
             def _():
-                side_copy(src, dst, ssem, rsem, side).wait_send()
+                side_copy(src, dst, ssem, rsem, side, number).wait_send()
                 pltpu.make_async_remote_copy(
-                    src_ref=src.at[1 - side], dst_ref=dst.at[side],
+                    src_ref=src.at[1 - side, pl.ds(0, number)], dst_ref=dst.at[side, pl.ds(0, number)],
                     send_sem=ssem.at[1 - side], recv_sem=rsem.at[side],
                     device_id={"space": me - 1 if side == 0 else me + 1},
                     device_id_type=pl.DeviceIdType.MESH,
                 ).wait_recv()
 
+    def ring(h):
+        return msg_ref.at[h], got_ref.at[h], send1.at[h], recv1.at[h]
+
+    def zring(h):
+        return zmsg_ref.at[h], zgot_ref.at[h], send2.at[h], recv2.at[h], pairs + (0 if h else tiles)
+
     if few:
         greeted(barrier)
     else:
         pl.semaphore_wait(barrier, last)
-    send(msg_ref, got_ref, send1, recv1)
+    send(*ring(0))
 
     whole(reals_ref, 3).wait()
     whole(flags_ref, 4).wait()
@@ -186,6 +199,7 @@
             tmsg_ref[side, c:c + 1, :] = te_ref[side, cut.start:cut.start + 1, :]
             tmsg_ref[side, tiles + c:tiles + c + 1, :] = te_ref[side, cut.stop - 1:cut.stop, :]
     send(bmsg_ref, bgot_ref, sendb, recvb)
+    send(*ring(1))
     send(tmsg_ref, tgot_ref, sendt, recvt)
 
     def edge(a, b, v, u):
@@ -281,7 +295,7 @@
         apply_part(q_ref, w_ref, 0, s, None, (q_ref, 1))
         apply_part(q_ref, w_ref, rows - 1, s, (q_ref, rows - 2), None)
 
-    done(msg_ref, got_ref, send1, recv1)
+    done(*ring(0))
     if few:
         greet(hello)
     done(bmsg_ref, bgot_ref, sendb, recvb)
@@ -291,48 +305,51 @@
 
     halo_a = [row_of(side, tiles) for side in range(2)]
     halo_v = [row_of(side, 2 * tiles) for side in range(2)]
+    over = []
     for side, r in ends:
         i = 1 + side
-        h = edge(active[r:r + 1, :], halo_a[side], valid[r:r + 1, :], halo_v[side])
-        wts_ref[r, i:i + 1, :] = h
-        wts_ref[r, 0:1, :] += h
-        wts_ref[r, 5:6, :] += 0.5 * h
-        va = got_ref[side, 0:pairs, :]
-        vb = got_ref[side, pairs:2 * pairs, :]
-        dots = jnp.zeros((pairs, LANES), F32)
-        for c, cut in enumerate(cuts):
-            common = bgot_ref[side, c:c + 1, :]
-            qh = jnp.where(tile_a == c, va, 0.0) + jnp.where(tile_b == c, vb, 0.0)
-            qhalo_ref[side, :, cut] = qh
-            q0 = q_ref[r, :pairs, cut]
-            w0 = w_ref[r, :pairs, cut] + h[:, cut] * (q0 - (qh + common))
-            w_ref[r, :pairs, cut] = w0
-            w_ref[r, extra, cut] += h[:, cut] * (q_ref[r, extra, cut] - common)
-            dots = dots + q0 * w0
-        acc_ref[1] += dots
+        x = edge(active[r:r + 1, :], halo_a[side], valid[r:r + 1, :], halo_v[side])
+        over.append(x)
+        wts_ref[r, i:i + 1, :] = x
+        wts_ref[r, 0:1, :] += x
+        wts_ref[r, 5:6, :] += 0.5 * x
 
     def precond_row(r):
         for c, cut in enumerate(cuts):
             z_ref[r, :, cut] = product(w_ref[r, :, cut], r, c)
 
-    def pack(src, r, dst, side):
-        va = src[r, :pairs, 0:LANES]
-        vb = va
-        for c in range(1, tiles):
-            x = src[r, :pairs, cuts[c]]
-            va = jnp.where(tile_a == c, x, va)
-            vb = jnp.where(tile_b == c, x, vb)
-        dst[side, 0:pairs, :] = va
-        dst[side, pairs:2 * pairs, :] = vb
-        for c, cut in enumerate(cuts):
-            dst[side, 2 * pairs + c:2 * pairs + c + 1, :] = src[r, pairs:pairs + 1, cut]
-
-    precond_row(0)
-    precond_row(rows - 1)
-    for side, r in ends:
-        pack(z_ref, r, zmsg_ref, side)
-    send(zmsg_ref, zgot_ref, send2, recv2)
-
+    for h, s in halves:
+        if h:
+            done(*ring(h))
+        for side, r in ends:
+            va = got_ref[h, side, 0:piece, :]
+            vb = got_ref[h, side, piece:pairs, :]
+            last_a = last_b = None
+            dots = jnp.zeros((piece, LANES), F32)
+            for c, cut in enumerate(cuts):
+                common = bgot_ref[side, c:c + 1, :]
+                qh = jnp.where(tile_a[s] == c, va, 0.0) + jnp.where(tile_b[s] == c, vb, 0.0)
+                qhalo_ref[side, s, cut] = qh
+                q0 = q_ref[r, s, cut]
+                w0 = w_ref[r, s, cut] + over[side][:, cut] * (q0 - (qh + common))
+                w_ref[r, s, cut] = w0
+                dots = dots + q0 * w0
+                if h == 0:
+                    we = w_ref[r, extra, cut] + over[side][:, cut] * (q_ref[r, extra, cut] - common)
+                    w_ref[r, extra, cut] = we
+                    z = product(jnp.concatenate([w0, we], 0), r, c)
+                    z_ref[r, extra, cut] = z[piece:]
+                    zmsg_ref[h, side, pairs + c:pairs + c + 1, :] = z[piece:piece + 1]
+                    z = z[:piece]
+                else:
+                    z = product(w0, r, c)
+                z_ref[r, s, cut] = z
+                last_a = z if c == 0 else jnp.where(tile_a[s] == c, z, last_a)
+                last_b = z if c == 0 else jnp.where(tile_b[s] == c, z, last_b)
+            acc_ref[1, s, :] += dots
+            zmsg_ref[h, side, 0:piece, :] = last_a
+            zmsg_ref[h, side, piece:pairs, :] = last_b
+        send(*zring(h))
 
     def moment_part(r, s, north):
         mu = nu = None
@@ -406,19 +423,20 @@
         for c, cut in enumerate(cuts):
             zhalo_ref[side, :, cut] = near[c]
 
-    done(zmsg_ref, zgot_ref, send2, recv2)
-    coupling = []
-    for side, r in ends:
-        va = zgot_ref[side, 0:pairs, :]
-        vb = zgot_ref[side, pairs:2 * pairs, :]
-        total = jnp.zeros((pairs, LANES), F32)
-        for c, cut in enumerate(cuts):
-            other = zgot_ref[side, 2 * pairs + c:2 * pairs + c + 1, :] + zhalo_ref[side, :, cut]
-            zh = jnp.where(tile_a == c, va, jnp.where(tile_b == c, vb, other))
-            zhalo_ref[side, :, cut] = zh
-            total = total + wts_ref[r, 1 + side:2 + side, cut] * z_ref[r, :pairs, cut] * zh
-        coupling.append(total)
-    late = lines(coupling)
+    coupling = [[], []]
+    for h, s in halves:
+        done(*zring(h))
+        for side, r in ends:
+            va = zgot_ref[h, side, 0:piece, :]
+            vb = zgot_ref[h, side, piece:pairs, :]
+            joined = jnp.zeros((piece, LANES), F32)
+            for c, cut in enumerate(cuts):
+                other = zgot_ref[0, side, pairs + c:pairs + c + 1, :] + zhalo_ref[side, s, cut]
+                zh = jnp.where(tile_a[s] == c, va, jnp.where(tile_b[s] == c, vb, other))
+                zhalo_ref[side, s, cut] = zh
+                joined = joined + over[side][:, cut] * z_ref[r, s, cut] * zh
+            coupling[side].append(joined)
+    late = lines([jnp.concatenate(x, 0) for x in coupling])
     late_ref[...] = late
     def late_copy(k):
         return pltpu.make_async_remote_copy(
@@ -512,10 +530,10 @@
     field = jax.ShapeDtypeStruct((rows, ext, cols), F32)
     vm = pl.BlockSpec(memory_space=pltpu.VMEM)
     hbm = pl.BlockSpec(memory_space=pltpu.HBM)
-    msg = (2, 2 * pairs, LANES)
+    msg = (2, 2, pairs, LANES)
     bmsg = (2, 3 * tiles, LANES)
     tmsg = (2, 2 * tiles, LANES)
-    zmsg = (2, 2 * pairs + tiles, LANES)
+    zmsg = (2, 2, pairs + tiles, LANES)
     others = count - 1
     r0, q, w, z, y, coef = pl.pallas_call(
         functools.partial(krylov_kernel, count),
@@ -537,7 +555,9 @@
             *[pltpu.VMEM(shape, F32) for shape in (msg, bmsg, tmsg, zmsg) for _ in range(2)],
             pltpu.VMEM((4, pairs, LANES), F32),
             *[pltpu.VMEM(shape, F32) for _ in range(2) for shape in ((8, LANES), (others, 8, LANES))],
-            *[pltpu.SemaphoreType.DMA((2,))] * 8,
+            *[pltpu.SemaphoreType.DMA((2, 2))] * 2,
+            *[pltpu.SemaphoreType.DMA((2,))] * 4,
+            *[pltpu.SemaphoreType.DMA((2, 2))] * 2,
             *[pltpu.SemaphoreType.DMA] * 2,
             *[pltpu.SemaphoreType.DMA((others,))] * 2,
             pltpu.SemaphoreType.DMA((6,)),

time: 18.6 us -> 18.6 us (level)
  no operation moved by 1% of the time
where the time goes in v7:
time: 18.6 us; the launch traced here: 18.4 us
  Pallas kernels  17.8 us (96%)
  between operations  0.64 us (3%)
    pallas_call x1, Pallas kernels, on_device(): pl.pallas_call(functools.partial(krylov_kernel, count), out_shape=[field]...  15.5 us
    pallas_call x1, Pallas kernels, on_device(): pl.pallas_call(combine_kernel, out_shape=[out, out], in_specs=[vm] * 6, o...  2.25 us

profile of v7, /device:TPU:0, one launch (start us, length us, event | category | flops | bytes accessed | tf_op | source)
XLA Modules:
  0.0 18.4 jit_solution(5472630056137317199)
XLA Ops:
  0.6 15.5 %krylov.1 = (f32[8,72,1024]{2,1,0:T(8,128)S(1)}, f32[8,72,1024]{2,1,0:T(8,128)S(1)}, f32[8,72,1024]{2,1,0:T(8,128)S(1)}, f32[8,72,1024]{2,1,0:T(8,128)S(1)}, f32...) custom-call(f32[8,1024]{1,0:T(8,128)} %cond_hbm.1, s32[8,1024]{1,0:T(8,128)} %nodata_hbm.1, s32[8,1024]{1,0:T(8,128)} %gmask_hbm.1, ...), custom_call_target="tpu_custom_call" | custom-call | tf_op jit(solution)/shard_map/krylov/pallas_call | solution.py:538
  16.1 2.3 %combine.1 = (f32[64,8,1024]{2,1,0:T(8,128)}, f32[64,8,1024]{2,1,0:T(8,128)}) custom-call(f32[2,64,128]{2,1,0:T(8,128)S(1)} %get-tuple-element.8.coef_ref, f32[8,72,1024]{2,1,0:T(8,128)S(1)} %get-tuple-element.9.r0_ref, f32[8,72,1024]{2,1,0:T(8,128)S(1)} %get-tuple-element.10.q_ref, f32[8,72,1024]{2,1,0:T(8,128)S(1)} %get-tuple-element.11.w_ref, ...), custom_call_target="tpu_custom_call" | custom-call | tf_op jit(solution)/shard_map/combine/pallas_call | solution.py:576

commit v8 on v7

--- a/solution.py
+++ b/solution.py
@@ -294,6 +294,15 @@
     for s in (*parts, extra):
         apply_part(q_ref, w_ref, 0, s, None, (q_ref, 1))
         apply_part(q_ref, w_ref, rows - 1, s, (q_ref, rows - 2), None)
+
+    def image_row(r):
+        for s in parts:
+            apply_part(q_ref, w_ref, r, s, (q_ref, r - 1), (q_ref, r + 1), 1)
+        apply_part(q_ref, w_ref, r, extra, (q_ref, r - 1), (q_ref, r + 1))
+
+    ready = rows - 2 - 3
+    for r in range(ready + 1, rows - 1):
+        image_row(r)
 
     done(*ring(0))
     if few:
@@ -362,18 +371,13 @@
         acc_ref[2, s, :] += mu
         acc_ref[3, s, :] += nu
 
-    def image_row(r):
-        for s in parts:
-            apply_part(q_ref, w_ref, r, s, (q_ref, r - 1), (q_ref, r + 1), 1)
-        apply_part(q_ref, w_ref, r, extra, (q_ref, r - 1), (q_ref, r + 1))
-
     def moment_row(r):
         for s in parts:
             moment_part(r, s, r > 0)
 
     image_row(1)
     for r in inner:
-        if r + 1 in inner:
+        if r + 1 <= ready:
             image_row(r + 1)
         precond_row(r)
         moment_row(r - 1)

time: 18.6 us -> 18.2 us (0.978)
  Pallas kernels: 17.8 us -> 17.4 us
    pallas_call x1, Pallas kernels: 15.5 us -> 15.2 us  [on_device(): pl.pallas_call(functools.partial(krylov_kernel, count), out_shape=[field]...]
where the time goes in v8:
time: 18.2 us; the launch traced here: 18.1 us
  Pallas kernels  17.4 us (96%)
  between operations  0.64 us (4%)
    pallas_call x1, Pallas kernels, on_device(): pl.pallas_call(functools.partial(krylov_kernel, count), out_shape=[field]...  15.2 us
    pallas_call x1, Pallas kernels, on_device(): pl.pallas_call(combine_kernel, out_shape=[out, out], in_specs=[vm] * 6, o...  2.25 us

profile of v8, /device:TPU:0, one launch (start us, length us, event | category | flops | bytes accessed | tf_op | source)
XLA Modules:
  0.0 18.1 jit_solution(3838088795184864027)
XLA Ops:
  0.6 15.2 %krylov.1 = (f32[8,72,1024]{2,1,0:T(8,128)S(1)}, f32[8,72,1024]{2,1,0:T(8,128)S(1)}, f32[8,72,1024]{2,1,0:T(8,128)S(1)}, f32[8,72,1024]{2,1,0:T(8,128)S(1)}, f32...) custom-call(f32[8,1024]{1,0:T(8,128)} %cond_hbm.1, s32[8,1024]{1,0:T(8,128)} %nodata_hbm.1, s32[8,1024]{1,0:T(8,128)} %gmask_hbm.1, ...), custom_call_target="tpu_custom_call" | custom-call | tf_op jit(solution)/shard_map/krylov/pallas_call | solution.py:542
  15.8 2.3 %combine.1 = (f32[64,8,1024]{2,1,0:T(8,128)}, f32[64,8,1024]{2,1,0:T(8,128)}) custom-call(f32[2,64,128]{2,1,0:T(8,128)S(1)} %get-tuple-element.8.coef_ref, f32[8,72,1024]{2,1,0:T(8,128)S(1)} %get-tuple-element.9.r0_ref, f32[8,72,1024]{2,1,0:T(8,128)S(1)} %get-tuple-element.10.q_ref, f32[8,72,1024]{2,1,0:T(8,128)S(1)} %get-tuple-element.11.w_ref, ...), custom_call_target="tpu_custom_call" | custom-call | tf_op jit(solution)/shard_map/combine/pallas_call | solution.py:580

commit v9 on v8

--- a/solution.py
+++ b/solution.py
@@ -441,10 +441,12 @@
                 joined = joined + over[side][:, cut] * z_ref[r, s, cut] * zh
             coupling[side].append(joined)
     late = lines([jnp.concatenate(x, 0) for x in coupling])
-    late_ref[...] = late
+    for i in range(2):
+        late_ref[i] = late[i:i + 1, :]
     def late_copy(k):
+        row = jnp.where(me + k < count, 0, 1)
         return pltpu.make_async_remote_copy(
-            src_ref=late_ref, dst_ref=lates_ref.at[k - 1], send_sem=send4.at[k - 1], recv_sem=recv4.at[k - 1],
+            src_ref=late_ref.at[row], dst_ref=lates_ref.at[k - 1], send_sem=send4.at[k - 1], recv_sem=recv4.at[k - 1],
             device_id={"space": lax.rem(me + k, count)}, device_id_type=pl.DeviceIdType.MESH,
         )
 
@@ -491,7 +493,7 @@
         def _():
             late_copy(k).wait_recv()
     for k in range(1, count):
-        joint = joint + jnp.where(k <= me, lates_ref[k - 1, 0:1, :], lates_ref[k - 1, 1:2, :])
+        joint = joint + lates_ref[k - 1]
     a1 = gamma1 / (known - scale * joint)
     first = a0 + a1 * (1.0 + beta)
     both = jnp.concatenate([first, a0 * a1, jnp.zeros((6, LANES), F32)], 0).T
@@ -558,7 +560,7 @@
             pltpu.VMEM((2, pairs, cols), F32),
             *[pltpu.VMEM(shape, F32) for shape in (msg, bmsg, tmsg, zmsg) for _ in range(2)],
             pltpu.VMEM((4, pairs, LANES), F32),
-            *[pltpu.VMEM(shape, F32) for _ in range(2) for shape in ((8, LANES), (others, 8, LANES))],
+            *[pltpu.VMEM(shape, F32) for shape in ((8, LANES), (others, 8, LANES), (2, 1, LANES), (others, 1, LANES))],
             *[pltpu.SemaphoreType.DMA((2, 2))] * 2,
             *[pltpu.SemaphoreType.DMA((2,))] * 4,
             *[pltpu.SemaphoreType.DMA((2, 2))] * 2,

time: 18.2 us -> 18.2 us (level)
  no operation moved by 1% of the time
where the time goes in v9:
time: 18.2 us; the launch traced here: 18 us
  Pallas kernels  17.4 us (96%)
  between operations  0.64 us (4%)
    pallas_call x1, Pallas kernels, on_device(): pl.pallas_call(functools.partial(krylov_kernel, count), out_shape=[field]...  15.1 us
    pallas_call x1, Pallas kernels, on_device(): pl.pallas_call(combine_kernel, out_shape=[out, out], in_specs=[vm] * 6, o...  2.25 us

profile of v9, /device:TPU:0, one launch (start us, length us, event | category | flops | bytes accessed | tf_op | source)
XLA Modules:
  0.0 18.0 jit_solution(6234057367875866814)
XLA Ops:
  0.6 15.1 %krylov.1 = (f32[8,72,1024]{2,1,0:T(8,128)S(1)}, f32[8,72,1024]{2,1,0:T(8,128)S(1)}, f32[8,72,1024]{2,1,0:T(8,128)S(1)}, f32[8,72,1024]{2,1,0:T(8,128)S(1)}, f32...) custom-call(f32[8,1024]{1,0:T(8,128)} %cond_hbm.1, s32[8,1024]{1,0:T(8,128)} %nodata_hbm.1, s32[8,1024]{1,0:T(8,128)} %gmask_hbm.1, ...), custom_call_target="tpu_custom_call" | custom-call | tf_op jit(solution)/shard_map/krylov/pallas_call | solution.py:544
  15.8 2.3 %combine.1 = (f32[64,8,1024]{2,1,0:T(8,128)}, f32[64,8,1024]{2,1,0:T(8,128)}) custom-call(f32[2,64,128]{2,1,0:T(8,128)S(1)} %get-tuple-element.8.coef_ref, f32[8,72,1024]{2,1,0:T(8,128)S(1)} %get-tuple-element.9.r0_ref, f32[8,72,1024]{2,1,0:T(8,128)S(1)} %get-tuple-element.10.q_ref, f32[8,72,1024]{2,1,0:T(8,128)S(1)} %get-tuple-element.11.w_ref, ...), custom_call_target="tpu_custom_call" | custom-call | tf_op jit(solution)/shard_map/combine/pallas_call | solution.py:582
